TPU v7x, 32 devices: a whole 2x2x4 slice. The times are simulated.
32 devices in a mesh: gx: 4 (over y, x), gy: 8 (over z, core).
Axes of the slice: x: 2, y: 2, z: 4, core: 2. Of those that a mesh axis runs over, the one named last changes fastest.
Arguments:
- cotangent: float32 [128, 512, 128], P('gx', 'gy'), may hold values from -6 to 6
- speed: float32 [3, 128, 512, 128], P(None, 'gx', 'gy'), may hold values from 0.05 to 0.45
- coeff: float32 [3, 128, 512, 128], P(None, 'gx', 'gy'), may hold values from 0.3 to 3
- dirs: int32 [3, 128, 512], P(None, 'gx', 'gy'), may hold values from 0 to 1
Outputs:
- grad: float32 [128, 512, 128], P('gx', 'gy')
Inputs may be any that keep to these rules, and one draw needn't show every extreme that they name: `dirs`: 0 means the lower cell of a face is upwind, 1 the upper cell.
All inputs are finite; a program needn't handle non-finite values.
Results may differ from a plain program's by a relative error of at most 0.0003.
Values sent between devices are 32-bit elements; how exact they have to be, the bound alone decides.
A program may use at most 128 MiB of HBM per device.

v0:
```python
import functools

import jax
import jax.numpy as jnp
from jax import lax
from jax.experimental import pallas as pl
from jax.experimental.pallas import tpu as pltpu
from jax.sharding import PartitionSpec as P

explicit_table = (
    (0.0, 0.0, 0.0, 0.0),
    (0.5, 0.0, 0.0, 0.0),
    (0.25, 0.5, 0.0, 0.0),
    (0.2, 0.3, 0.5, 0.0),
)
implicit_table = (
    (0.0, 0.0, 0.0, 0.0),
    (0.25, 0.25, 0.0, 0.0),
    (0.25, 0.25, 0.25, 0.0),
    (0.15, 0.35, 0.25, 0.25),
)
section_weights = (0.15, 0.35, 0.25, 0.25)
implicit_diagonal = 0.25

MESH = pl.DeviceIdType.MESH
PAD = 8


GROUP = {"masks": 4, "diagonals": 2, "source": 2, "next": 2, "image": 2, "energy": 4, "carry": 4, "both": 2, "gather": 2}


def grouped(name, low, high, value, store, carry):
    size = GROUP[name]

    def group(planes, carry):
        found = []
        for x in planes:
            carry, kept = value(x, carry)
            found.append(kept)
        for x, kept in zip(planes, found):
            store(x, kept)
        return carry

    turns = (high - low) // size
    carry = lax.fori_loop(
        0, turns, lambda t, c: group([low + t * size + k for k in range(size)], c), carry)
    rest = list(range(low + turns * size, high))
    return group(rest, carry) if rest else carry


def kernel(
    gx, gy, cot_hbm, speed_hbm, coeff_hbm, dirs_ref, out_ref,
    f0, f1, f2, f3, f4, f5, f6, fr0, fr1, fr2, fw0, fw1, fw2, dw0, dw1, dw2, base, cx, cy, cz, czm, px, py, pz, mx, my, mz, gdiag, fdiag,
    ysend, yrecv, landed, stage, red_y, red_x, load_sem, send_sem, recv_sem, rys, ryr, rxs, rxr,
):
    nx, ny, nz = out_ref.shape
    fields = (f0, f1, f2, f3, f4, f5, f6)
    fr, fw, dw = (fr0, fr1, fr2), (fw0, fw1, fw2), (dw0, dw1, dw2)
    me_x, me_y = lax.axis_index("gx"), lax.axis_index("gy")
    own = pl.ds(PAD, ny)
    up = pl.ds(PAD + 1, ny)
    down = pl.ds(PAD - 1, ny)
    lane = lax.broadcasted_iota(jnp.int32, (ny, nz), 1)
    last_lane = lane == nz - 1

    def ahead_z(v):
        return pltpu.roll(v, nz - 1, 1)

    def behind_z(v):
        return pltpu.roll(v, 1, 1)

    loads = [
        pltpu.make_async_copy(src, dst, load_sem.at[k])
        for k, (src, dst) in enumerate((
            (speed_hbm.at[0], px),
            (speed_hbm.at[1], py),
            (speed_hbm.at[2], pz),
            (coeff_hbm.at[0], cx.at[pl.ds(1, nx)]),
            (coeff_hbm.at[1], cy.at[:, own]),
            (coeff_hbm.at[2], cz),
            (cot_hbm, fields[0].at[pl.ds(1, nx), own]),
        ))
    ]
    for load in loads:
        load.start()

    plane = jnp.zeros((ny, nz), jnp.float32)
    for k in range(7):
        fields[k][0, own] = plane
        fields[k][nx + 1, own] = plane
    cx[0] = plane
    mx[0] = plane
    landed[0] = plane
    landed[1] = plane
    yrecv[...] = jnp.zeros_like(yrecv)

    def zero_rows(x, carry):
        cy[x, pl.ds(0, PAD)] = jnp.zeros((PAD, nz), jnp.float32)
        my[x, pl.ds(0, PAD)] = jnp.zeros((PAD, nz), jnp.float32)
        for k in range(1, 7):
            fields[k][x + 1, pl.ds(0, PAD)] = jnp.zeros((PAD, nz), jnp.float32)
            fields[k][x + 1, pl.ds(PAD + ny, PAD)] = jnp.zeros((PAD, nz), jnp.float32)
        return carry

    lax.fori_loop(0, nx, zero_rows, 0)

    barrier = pltpu.get_barrier_semaphore()
    for off in range(1, gx):
        pl.semaphore_signal(barrier, inc=1, device_id={"gx": lax.rem(me_x + off, gx)}, device_id_type=MESH)
    for off in range(1, gy):
        pl.semaphore_signal(barrier, inc=1, device_id={"gy": lax.rem(me_y + off, gy)}, device_id_type=MESH)
    pl.semaphore_wait(barrier, gx + gy - 2)

    def x_down(tag, src, dst):
        return pltpu.make_async_remote_copy(
            src, dst, send_sem.at[tag, 0], recv_sem.at[tag, 0],
            device_id={"gx": lax.rem(me_x + gx - 1, gx)}, device_id_type=MESH)

    def x_up(tag, src, dst):
        return pltpu.make_async_remote_copy(
            src, dst, send_sem.at[tag, 1], recv_sem.at[tag, 1],
            device_id={"gx": lax.rem(me_x + 1, gx)}, device_id_type=MESH)

    def y_down(tag):
        return pltpu.make_async_remote_copy(
            ysend.at[tag, 0], yrecv.at[tag, 1], send_sem.at[tag, 2], recv_sem.at[tag, 2],
            device_id={"gy": lax.rem(me_y + gy - 1, gy)}, device_id_type=MESH)

    def y_up(tag):
        return pltpu.make_async_remote_copy(
            ysend.at[tag, 1], yrecv.at[tag, 0], send_sem.at[tag, 3], recv_sem.at[tag, 3],
            device_id={"gy": lax.rem(me_y + 1, gy)}, device_id_type=MESH)

    def copies(tag):
        field = fields[tag]
        return (
            x_down(tag, field.at[1, own], field.at[nx + 1, own]),
            x_up(tag, field.at[nx, own], field.at[0, own]),
            y_down(tag),
            y_up(tag),
        )

    low_x, low_y = me_x > 0, me_y > 0
    high_x, high_y = me_x < gx - 1, me_y < gy - 1

    def start_x(tag):
        xd, xu, _, _ = copies(tag)
        pl.when(low_x)(xd.start)
        pl.when(high_x)(xu.start)

    def start_y(tag):
        _, _, yd, yu = copies(tag)
        pl.when(low_y)(yd.start)
        pl.when(high_y)(yu.start)

    def arrive(tag):
        xd, xu, yd, yu = copies(tag)
        pl.when(high_y)(yd.wait_recv)
        pl.when(low_y)(yu.wait_recv)
        pl.when(high_x)(xd.wait_recv)
        pl.when(low_x)(xu.wait_recv)

    def sent(tag):
        xd, xu, yd, yu = copies(tag)
        pl.when(low_x)(xd.wait_send)
        pl.when(high_x)(xu.wait_send)
        pl.when(low_y)(yd.wait_send)
        pl.when(high_y)(yu.wait_send)

    def unpack(tag):
        for x in range(nx):
            fields[tag][1 + x, pl.ds(PAD - 1, 1)] = yrecv[tag, 0, pl.ds(x, 1)]
            fields[tag][1 + x, pl.ds(PAD + ny, 1)] = yrecv[tag, 1, pl.ds(x, 1)]

    for load in loads:
        load.wait()

    for x in range(nx):
        at = pl.ds(x, 1)
        ysend[0, 0, at] = fields[0][x + 1, pl.ds(PAD, 1)]
        ysend[0, 1, at] = fields[0][x + 1, pl.ds(PAD + ny - 1, 1)]
        ysend[7, 1, at] = cy[x, pl.ds(PAD + ny - 1, 1)]
        ysend[8, 1, at] = py[x, pl.ds(ny - 1, 1)]
    dirs = [dirs_ref[d].astype(jnp.float32).T for d in range(3)]
    edge = jnp.broadcast_to(dirs_ref[1][:, ny - 1:], (nx, nz))
    ysend[8, 1] = jnp.where(edge > 0, ysend[8, 1], 0.0)

    def upper(d, x):
        column = (lax.broadcasted_iota(jnp.int32, (nx, nz), 0) == x).astype(jnp.float32)
        return jnp.dot(dirs[d], column, preferred_element_type=jnp.float32) > 0.5

    stage[...] = jnp.where(upper(0, nx - 1), px[nx - 1], 0.0)
    start_x(0)
    start_y(0)
    statics = (
        (x_up(7, cx.at[nx], landed.at[0]), y_up(7)),
        (x_up(8, stage, landed.at[1]), y_up(8)),
    )
    for xu, yu in statics:
        pl.when(high_x)(xu.start)
        pl.when(high_y)(yu.start)

    def masks(x, carry):
        low = [jnp.where(upper(d, x), ref[x], 0.0) for d, ref in enumerate((px, py, pz))]
        return carry, (low, [ref[x] - m for m, ref in zip(low, (px, py, pz))], cz[x])

    def store_masks(x, kept):
        low, high, c = kept
        mx[x + 1] = low[0]
        my[x, own] = low[1]
        mz[x] = jnp.where(last_lane, 0.0, low[2])
        px[x], py[x] = high[0], high[1]
        pz[x] = high[2]
        czm[x] = jnp.where(last_lane, 0.0, c)

    grouped("masks", 0, nx, masks, store_masks, 0)

    def diagonals(x, carry):
        p = pz[x]
        f = px[x] + mx[x] + py[x] + my[x, down] + p + behind_z(mz[x])
        g = cx[x + 1] + cx[x] + cy[x, own] + cy[x, down] + cz[x] + behind_z(czm[x])
        return carry, (f, g, jnp.where(last_lane, 0.0, p))

    def store_diagonals(x, kept):
        fdiag[x], gdiag[x], pz[x] = kept

    grouped("diagonals", 0, nx, diagonals, store_diagonals, 0)

    arrive(0)
    for xu, yu in statics:
        pl.when(low_x)(xu.wait_recv)
        pl.when(low_y)(yu.wait_recv)
    unpack(0)
    cx[0] = landed[0]
    mx[0] = landed[1]
    gdiag[0] += cx[0]
    fdiag[0] += mx[0]
    first = pl.ds(0, 1)
    for x in range(nx):
        row = yrecv[7, 0, pl.ds(x, 1)]
        cy[x, pl.ds(PAD - 1, 1)] = row
        gdiag[x, first] += row
        row = yrecv[8, 0, pl.ds(x, 1)]
        my[x, pl.ds(PAD - 1, 1)] = row
        fdiag[x, first] += row

    def spread(ref, x):
        v = ref[x + 1, own]
        total = cx[x + 1] * ref[x + 2, own] + cx[x] * ref[x, own]
        total += cy[x, own] * ref[x + 1, up] + cy[x, down] * ref[x + 1, down]
        c = czm[x]
        total += c * ahead_z(v) + behind_z(c * v)
        return v, total - gdiag[x] * v

    def carried(ref, x):
        v = ref[x + 1, own]
        total = px[x] * ref[x + 2, own] + mx[x] * ref[x, own]
        total += py[x] * ref[x + 1, up] + my[x, down] * ref[x + 1, down]
        total += pz[x] * ahead_z(v) + behind_z(mz[x] * v)
        return total - fdiag[x] * v

    def fold(v):
        return jnp.sum(v.reshape(v.shape[0] // 8, 8, nz), axis=0)

    nothing = jnp.zeros((8, nz), jnp.float32)

    def keep(tag, x, v):
        fields[tag][x + 1, own] = v
        ysend[tag, 0, pl.ds(x, 1)] = v[:1]
        ysend[tag, 1, pl.ds(x, 1)] = v[ny - 1:]

    def across(step, slots, axis, me, count, send, recv):
        out = [
            pltpu.make_async_remote_copy(
                slots.at[step, me], slots.at[step, me], send.at[step, off], recv.at[step, me],
                device_id={axis: lax.rem(me + off, count)}, device_id_type=MESH)
            for off in range(1, count)
        ]
        for copy in out:
            copy.start()

        def result():
            for off in range(1, count):
                peer = lax.rem(me + off, count)
                pltpu.make_async_remote_copy(
                    slots.at[step, peer], slots.at[step, peer], send.at[step, off], recv.at[step, peer],
                    device_id={axis: peer}, device_id_type=MESH).wait_recv()
            total = slots[step, 0]
            for k in range(1, count):
                total = total + slots[step, k]
            return total

        return out, result

    row_x = lax.broadcasted_iota(jnp.int32, (nx, nz), 0)
    between = jnp.logical_and(row_x > 0, row_x < nx - 1)
    pending = []
    for step, section in enumerate((3, 2, 1)):
        r_tag, w_tag = 1 + step, 4 + step
        r_ref, w_ref = fields[r_tag], fields[w_tag]

        def first_pass(x, m0):
            if step == 0:
                c_ref = fields[0]
                r = section_weights[3] * (spread(c_ref, x)[1] + carried(c_ref, x))
            else:
                r = following(x)
            r, more = r if step else (r, None)
            return m0 + fold(r * r), (r, more)

        def store_first(x, kept):
            r, more = kept
            keep(r_tag, x, r)
            if more is not None:
                fr[step - 1][x], dw[step - 1][x] = more

        m0 = nothing
        for x in (0, nx - 1):
            m0, kept = first_pass(x, m0)
            store_first(x, kept)
        start_x(r_tag)
        m0 = grouped("next" if step else "source", 1, nx - 1, first_pass, store_first, m0)
        start_y(r_tag)

        def second_pass(x, sums):
            m1, m2 = sums
            r, d = spread(r_ref, x)
            w = r - implicit_diagonal * d
            return (m1 + fold(r * w), m2 + fold(w * w)), w

        def store_second(x, w):
            keep(w_tag, x, w)

        sums = grouped("image", 1, nx - 1, second_pass, store_second, (nothing, nothing))
        arrive(r_tag)
        unpack(r_tag)
        for x in (0, nx - 1):
            sums, w = second_pass(x, sums)
            store_second(x, w)
        m1, m2 = sums
        start_x(w_tag)
        for side, face in ((0, yrecv[7, 0]), (1, ysend[7, 1])):
            change = jnp.where(between, -implicit_diagonal * face * yrecv[r_tag, side], 0.0)
            w = ysend[w_tag, side]
            ysend[w_tag, side] = w + change
            m1 += fold(ysend[r_tag, side] * change)
            m2 += fold((2.0 * w + change) * change)
        start_y(w_tag)
        for x in range(1, nx - 1):
            fields[w_tag][1 + x, pl.ds(PAD, 1)] = ysend[w_tag, 0, pl.ds(x, 1)]
            fields[w_tag][1 + x, pl.ds(PAD + ny - 1, 1)] = ysend[w_tag, 1, pl.ds(x, 1)]

        def third_pass(x, m3):
            w = w_ref[x + 1, own]
            jump_x = w_ref[x + 2, own] - w
            jump_y = w_ref[x + 1, up] - w
            jump_z = jnp.where(last_lane, 0.0, ahead_z(w)) - w
            total = cx[x + 1] * jump_x * jump_x + cy[x, own] * jump_y * jump_y
            total += cz[x] * jump_z * jump_z
            return m3 + fold(total), None

        m3 = grouped("energy", 0, nx - 1, third_pass, lambda x, kept: None, nothing)

        def store_r(x, kept):
            fr[step][x] = kept

        grouped("carry", 0, nx, lambda x, c: (c, carried(r_ref, x)), store_r, 0)
        arrive(w_tag)
        m3, _ = third_pass(nx - 1, m3)
        above = yrecv[w_tag, 1]
        m3 += fold(ysend[7, 1] * above * (above - 2.0 * ysend[w_tag, 1]))
        m3 = m2 + implicit_diagonal * m3
        rows = [jnp.sum(m, axis=0, keepdims=True) for m in (m0, m1, m2, m3)]
        red_y[step, me_y] = jnp.concatenate(rows + [jnp.zeros((4, nz), jnp.float32)], axis=0)
        out, result = across(step, red_y, "gy", me_y, gy, rys, ryr)
        pending += out
        unpack(w_tag)

        def store_w(x, kept):
            fw[step][x], dw[step][x] = kept

        grouped("both", 0, nx, lambda x, c: (c, (carried(w_ref, x), spread(w_ref, x)[1])), store_w, 0)
        red_x[step, me_x] = result()
        out, result = across(step, red_x, "gx", me_x, gx, rxs, rxr)
        pending += out

        target = section - 1
        share = section_weights[target] / section_weights[3]

        def gather(x, carry):
            total = share * fields[1][x + 1, own]
            for k in range(step):
                total += explicit_table[3 - k][target] * fr[k][x] + implicit_table[3 - k][target] * dw[k][x]
            if target == 0:
                total += fields[0][x + 1, own]
                for k in range(step):
                    on_r, on_w = weights[k]
                    total += on_r * fields[1 + k][x + 1, own] + on_w * fields[4 + k][x + 1, own]
            return carry, total

        if step == 0:
            weights = []
        def store_base(x, kept):
            base[x] = kept

        grouped("gather", 0, nx, gather, store_base, 0)

        total = result()
        total = jnp.broadcast_to(jnp.sum(total, axis=1, keepdims=True), (8, nz))
        m0, m1, m2, m3 = [total[k:k + 1] for k in range(4)]
        alpha = m0 / m1
        rr = alpha * alpha * m2 - m0
        ratio = rr / m0
        product = m1 - 2.0 * alpha * m2 + alpha * alpha * m3
        alpha_next = rr / (product - ratio * rr / alpha)
        on_r = alpha + alpha_next * (1.0 + ratio)
        on_w = -alpha_next * alpha
        weights.append((on_r, on_w))

        def following(x, step=step, section=section, target=target, on_r=on_r, on_w=on_w):
            r, w = fields[1 + step][x + 1, own], fields[4 + step][x + 1, own]
            advected = on_r * fr[step][x] + on_w * fw[step][x]
            diffused = (on_r / implicit_diagonal) * (r - w) + on_w * dw[step][x]
            total = base[x]
            total += explicit_table[section][target] * advected
            total += implicit_table[section][target] * diffused
            if target == 0:
                return total + on_r * r + on_w * w
            return total, (advected, diffused)

    def last(x, carry):
        out_ref[x] = following(x)
        return carry

    lax.fori_loop(0, nx, last, 0)
    for xu, yu in statics:
        pl.when(high_x)(xu.wait_send)
        pl.when(high_y)(yu.wait_send)
    for tag in range(7):
        sent(tag)
    for copy in pending:
        copy.wait_send()


def local(gx, gy, cotangent, speed, coeff, dirs):
    nx, ny, nz = cotangent.shape
    f32 = jnp.float32
    rows = ny + 2 * PAD
    plain = pltpu.VMEM((nx, ny, nz), f32)
    dma = pltpu.SemaphoreType.DMA
    anywhere = pl.BlockSpec(memory_space=pl.ANY)
    return pl.pallas_call(
        functools.partial(kernel, gx, gy),
        out_shape=jax.ShapeDtypeStruct((nx, ny, nz), f32),
        in_specs=[anywhere, anywhere, anywhere, pl.BlockSpec(memory_space=pltpu.VMEM)],
        out_specs=pl.BlockSpec(memory_space=pltpu.VMEM),
        scratch_shapes=[
            *[pltpu.VMEM((nx + 2, rows, nz), f32)] * 7,
            *[plain] * 9,
            plain,
            pltpu.VMEM((nx + 1, ny, nz), f32),
            pltpu.VMEM((nx, rows, nz), f32),
            plain, plain,
            plain, plain, plain,
            pltpu.VMEM((nx + 1, ny, nz), f32),
            pltpu.VMEM((nx, rows, nz), f32),
            plain,
            plain, plain,
            pltpu.VMEM((9, 2, nx, nz), f32),
            pltpu.VMEM((9, 2, nx, nz), f32),
            pltpu.VMEM((2, ny, nz), f32),
            pltpu.VMEM((ny, nz), f32),
            pltpu.VMEM((3, gy, 8, nz), f32),
            pltpu.VMEM((3, gx, 8, nz), f32),
            dma((7,)), dma((9, 4)), dma((9, 4)),
            dma((3, gy)), dma((3, gy)), dma((3, gx)), dma((3, gx)),
        ],
        compiler_params=pltpu.CompilerParams(
            collective_id=0, has_side_effects=True, vmem_limit_bytes=60 * 1024 * 1024
        ),
    )(cotangent, speed, coeff, dirs)


def solution(mesh):
    return jax.shard_map(
        functools.partial(local, mesh.shape["gx"], mesh.shape["gy"]),
        mesh=mesh,
        in_specs=(
            P("gx", "gy", None),
            P(None, "gx", "gy", None),
            P(None, "gx", "gy", None),
            P(None, "gx", "gy"),
        ),
        out_specs=P("gx", "gy", None),
        check_vma=False,
    )
```

profile of v0, /device:TPU:0, one launch (start us, length us, event | category | flops | bytes accessed | tf_op | source)
XLA Modules:
  0.0 60.2 jit_solution(2877154133265353162)
XLA Ops:
  0.0 57.9 %shard_map.46 = f32[32,64,128]{2,1,0:T(8,128)} custom-call(f32[32,64,128]{2,1,0:T(8,128)} %cot_hbm.1, f32[3,32,64,128]{3,2,1,0:T(8,128)} %speed_hbm.1, f32[3,32,64,128]{3,2,1,0:T(8,128)} %coeff_hbm.1, s32[3,32,64]{2,1,0:T(8,128)} %dirs_ref.1), custom_call_target="tpu_custom_call" | custom-call | tf_op jit(solution)/shard_map/pallas_call | solution.py:452
  57.9 2.3 %copy.6 = f32[32,64,128]{2,1,0:T(8,128)} copy(f32[32,64,128]{2,1,0:T(8,128)} %shard_map.46) | data formatting | bytes 2097152
where the time goes:
time: 60.4 us; the launch traced here: 60.2 us
  Pallas kernels  57.9 us (96%)
  local copies, waits for them, and re-layouts  2.31 us (4%)
    pallas_call x1, Pallas kernels, local(): pl.pallas_call(functools.partial(kernel, gx, gy), out_shape=jax.ShapeDtyp...  57.9 us
    unnamed x1, local copies, waits for them, and re-layouts  2.31 us

commit v1 on v0

v1 whole, which is shorter than its diff:
```python
import functools

import jax
import jax.numpy as jnp
from jax import lax
from jax.experimental import pallas as pl
from jax.experimental.pallas import tpu as pltpu
from jax.sharding import PartitionSpec as P

explicit_table = (
    (0.0, 0.0, 0.0, 0.0),
    (0.5, 0.0, 0.0, 0.0),
    (0.25, 0.5, 0.0, 0.0),
    (0.2, 0.3, 0.5, 0.0),
)
implicit_table = (
    (0.0, 0.0, 0.0, 0.0),
    (0.25, 0.25, 0.0, 0.0),
    (0.25, 0.25, 0.25, 0.0),
    (0.15, 0.35, 0.25, 0.25),
)
section_weights = (0.15, 0.35, 0.25, 0.25)
implicit_diagonal = 0.25

MESH = pl.DeviceIdType.MESH
PAD = 8


GROUP = {"masks": 4, "diagonals": 2, "source": 2, "next": 2, "image": 2, "energy": 4, "rim": 4, "carry": 4, "both": 2, "gather": 2}
CHUNKS = 4


def grouped(name, low, high, value, store, carry):
    size = GROUP[name]

    def group(planes, carry):
        found = []
        for x in planes:
            carry, kept = value(x, carry)
            found.append(kept)
        for x, kept in zip(planes, found):
            store(x, kept)
        return carry

    turns = (high - low) // size
    carry = lax.fori_loop(
        0, turns, lambda t, c: group([low + t * size + k for k in range(size)], c), carry)
    rest = list(range(low + turns * size, high))
    return group(rest, carry) if rest else carry


def kernel(
    gx, gy, cot_hbm, speed_hbm, coeff_hbm, dirs_ref, out_ref,
    f0, f1, f2, f3, f4, f5, f6, fr0, fr1, fr2, fw0, fw1, fw2, dw0, dw1, dw2, base, cx, cy, cz, czm, px, py, pz, mx, my, mz, gdiag, fdiag,
    ysend, yrecv, landed, wpart, ypart, yside, corner_out, corner_in, slots,
    load_sem, send_sem, recv_sem, corner_send, corner_recv, sum_send, sum_recv,
):
    nx, ny, nz = out_ref.shape
    fields = (f0, f1, f2, f3, f4, f5, f6)
    fr, fw, dw = (fr0, fr1, fr2), (fw0, fw1, fw2), (dw0, dw1, dw2)
    me_x, me_y = lax.axis_index("gx"), lax.axis_index("gy")
    count = gx * gy
    me = me_x * gy + me_y
    own = pl.ds(PAD, ny)
    up = pl.ds(PAD + 1, ny)
    down = pl.ds(PAD - 1, ny)
    lane = lax.broadcasted_iota(jnp.int32, (ny, nz), 1)
    last_lane = lane == nz - 1
    low_x, low_y = me_x > 0, me_y > 0
    high_x, high_y = me_x < gx - 1, me_y < gy - 1

    def ahead_z(v):
        return pltpu.roll(v, nz - 1, 1)

    def behind_z(v):
        return pltpu.roll(v, 1, 1)

    chunks = CHUNKS if nx % CHUNKS == 0 else 1
    piece = nx // chunks

    def load(k, src, dst):
        copy = pltpu.make_async_copy(src, dst, load_sem.at[k])
        copy.start()
        return copy

    with jax.named_scope("loads"):
        cot_load = load(0, cot_hbm, fields[0].at[pl.ds(1, nx), own])
        loads = []
        for chunk in range(chunks):
            at = pl.ds(chunk * piece, piece)
            loads.append([
                load(1 + 6 * chunk + k, src, dst)
                for k, (src, dst) in enumerate((
                    (coeff_hbm.at[0, at], cx.at[pl.ds(1 + chunk * piece, piece)]),
                    (coeff_hbm.at[1, at], cy.at[at, own]),
                    (coeff_hbm.at[2, at], cz.at[at]),
                    (speed_hbm.at[0, at], px.at[at]),
                    (speed_hbm.at[1, at], py.at[at]),
                    (speed_hbm.at[2, at], pz.at[at]),
                ))
            ])

        plane = jnp.zeros((ny, nz), jnp.float32)
        for k in range(7):
            fields[k][0, own] = plane
            fields[k][nx + 1, own] = plane
        landed[0] = plane
        landed[1] = plane
        yrecv[...] = jnp.zeros_like(yrecv)
        corner_in[...] = jnp.zeros_like(corner_in)

        barrier = pltpu.get_barrier_semaphore()
        for off in range(1, count):
            to = {"gx": lax.rem(me_x + off // gy, gx), "gy": lax.rem(me_y + off % gy, gy)}
            pl.semaphore_signal(barrier, inc=1, device_id=to, device_id_type=MESH)

        cx[0] = plane
        mx[0] = plane

        def zero_rows(x, carry):
            cy[x, pl.ds(0, PAD)] = jnp.zeros((PAD, nz), jnp.float32)
            my[x, pl.ds(0, PAD)] = jnp.zeros((PAD, nz), jnp.float32)
            for k in range(1, 7):
                fields[k][x + 1, pl.ds(0, PAD)] = jnp.zeros((PAD, nz), jnp.float32)
                fields[k][x + 1, pl.ds(PAD + ny, PAD)] = jnp.zeros((PAD, nz), jnp.float32)
            return carry

        lax.fori_loop(0, nx, zero_rows, 0)

    def channel(tag, k, src, dst, axis, move):
        size, at = (gx, me_x) if axis == "gx" else (gy, me_y)
        return pltpu.make_async_remote_copy(
            src, dst, send_sem.at[tag, k], recv_sem.at[tag, k],
            device_id={axis: lax.rem(at + size + move, size)}, device_id_type=MESH)

    def x_down(tag, src, dst):
        return channel(tag, 0, src, dst, "gx", -1)

    def x_up(tag, src, dst):
        return channel(tag, 1, src, dst, "gx", 1)

    def y_down(tag, src):
        return channel(tag, 2, src, yrecv.at[tag, 1], "gy", -1)

    def y_up(tag):
        return channel(tag, 3, ysend.at[tag, 1], yrecv.at[tag, 0], "gy", 1)

    def copies(tag):
        field = fields[tag]
        partial = tag > 3
        return (
            x_down(tag, wpart.at[tag - 4] if partial else field.at[1, own], field.at[nx + 1, own]),
            x_up(tag, field.at[nx, own], field.at[0, own]),
            y_down(tag, ypart.at[tag - 4] if partial else ysend.at[tag, 0]),
            y_up(tag),
        )

    starts = (low_x, high_x, low_y, high_y)
    ends = (high_x, low_x, high_y, low_y)

    def start(tag, *which):
        every = copies(tag)
        for k in which:
            pl.when(starts[k])(every[k].start)

    def arrive(tag, *which):
        every = copies(tag)
        for k in which:
            pl.when(ends[k])(every[k].wait_recv)

    def sent(tag):
        for k, copy in enumerate(copies(tag)):
            pl.when(starts[k])(copy.wait_send)

    XD, XU, YD, YU = range(4)

    def corners(step):
        out = []
        for k, (rows, dx, dy) in enumerate(((pl.ds(0, 1), -1, 1), (pl.ds(1, 2), -1, -1), (pl.ds(3, 1), 1, -1))):
            to = {"gx": lax.rem(me_x + gx + dx, gx), "gy": lax.rem(me_y + gy + dy, gy)}
            copy = pltpu.make_async_remote_copy(
                corner_out.at[step, rows], corner_in.at[step, rows],
                corner_send.at[step, k], corner_recv.at[step, k], device_id=to, device_id_type=MESH)
            toward = [low_x if dx < 0 else high_x, low_y if dy < 0 else high_y]
            whence = [high_x if dx < 0 else low_x, high_y if dy < 0 else low_y]
            out.append((copy, jnp.logical_and(*toward), jnp.logical_and(*whence)))
        return out

    def unpack(tag):
        for x in range(nx):
            fields[tag][1 + x, pl.ds(PAD - 1, 1)] = yrecv[tag, 0, pl.ds(x, 1)]
            fields[tag][1 + x, pl.ds(PAD + ny, 1)] = yrecv[tag, 1, pl.ds(x, 1)]

    with jax.named_scope("barrier"):
        cot_load.wait()
        for x in range(nx):
            at = pl.ds(x, 1)
            ysend[0, 0, at] = fields[0][x + 1, pl.ds(PAD, 1)]
            ysend[0, 1, at] = fields[0][x + 1, pl.ds(PAD + ny - 1, 1)]
        dirs = [dirs_ref[d].astype(jnp.float32).T for d in range(3)]
        pl.semaphore_wait(barrier, count - 1)
    start(0, XD, XU, YD, YU)

    def upper(d, x):
        column = (lax.broadcasted_iota(jnp.int32, (nx, nz), 0) == x).astype(jnp.float32)
        return jnp.dot(dirs[d], column, preferred_element_type=jnp.float32) > 0.5

    def masks(x, carry):
        low = [jnp.where(upper(d, x), ref[x], 0.0) for d, ref in enumerate((px, py, pz))]
        return carry, (low, [ref[x] - m for m, ref in zip(low, (px, py, pz))], cz[x])

    def store_masks(x, kept):
        low, high, c = kept
        at = pl.ds(x, 1)
        mx[x + 1] = low[0]
        my[x, own] = low[1]
        mz[x] = jnp.where(last_lane, 0.0, low[2])
        px[x], py[x] = high[0], high[1]
        pz[x] = high[2]
        czm[x] = jnp.where(last_lane, 0.0, c)
        ysend[8, 1, at] = low[1][ny - 1:]
        ysend[7, 1, at] = cy[x, pl.ds(PAD + ny - 1, 1)]

    def diagonals(x, carry):
        p = pz[x]
        f = px[x] + mx[x] + py[x] + my[x, down] + p + behind_z(mz[x])
        g = cx[x + 1] + cx[x] + cy[x, own] + cy[x, down] + cz[x] + behind_z(czm[x])
        return carry, (f, g, jnp.where(last_lane, 0.0, p))

    def store_diagonals(x, kept):
        fdiag[x], gdiag[x], pz[x] = kept

    for chunk in range(chunks):
        low, high = chunk * piece, (chunk + 1) * piece
        with jax.named_scope("loadwait"):
            for copy in loads[chunk]:
                copy.wait()
        with jax.named_scope("masks"):
            grouped("masks", low, high, masks, store_masks, 0)
        with jax.named_scope("diagonals"):
            grouped("diagonals", low, high, diagonals, store_diagonals, 0)

    statics = (
        (x_up(7, cx.at[nx], landed.at[0]), y_up(7)),
        (x_up(8, mx.at[nx], landed.at[1]), y_up(8)),
    )
    for xu, yu in statics:
        pl.when(high_x)(xu.start)
        pl.when(high_y)(yu.start)

    def spread(ref, x):
        v = ref[x + 1, own]
        total = cx[x + 1] * ref[x + 2, own] + cx[x] * ref[x, own]
        total += cy[x, own] * ref[x + 1, up] + cy[x, down] * ref[x + 1, down]
        c = czm[x]
        total += c * ahead_z(v) + behind_z(c * v)
        return v, total - gdiag[x] * v

    def inner(ref, x):
        v = ref[x + 1, own]
        total = cx[1] * ref[2, own] if x == 0 else cx[x] * ref[x, own]
        total += cy[x, own] * ref[x + 1, up] + cy[x, down] * ref[x + 1, down]
        c = czm[x]
        total += c * ahead_z(v) + behind_z(c * v)
        return v - implicit_diagonal * (total - gdiag[x] * v)

    def carried(ref, x):
        v = ref[x + 1, own]
        total = px[x] * ref[x + 2, own] + mx[x] * ref[x, own]
        total += py[x] * ref[x + 1, up] + my[x, down] * ref[x + 1, down]
        total += pz[x] * ahead_z(v) + behind_z(mz[x] * v)
        return total - fdiag[x] * v

    def fold(v):
        return jnp.sum(v.reshape(v.shape[0] // 8, 8, nz), axis=0)

    nothing = jnp.zeros((8, nz), jnp.float32)

    def keep(tag, x, v):
        fields[tag][x + 1, own] = v
        ysend[tag, 0, pl.ds(x, 1)] = v[:1]
        ysend[tag, 1, pl.ds(x, 1)] = v[ny - 1:]

    row_x = lax.broadcasted_iota(jnp.int32, (nx, nz), 0)
    between = jnp.logical_and(row_x > 0, row_x < nx - 1)
    across_x = jnp.where(high_x, implicit_diagonal, 0.0)
    across_y = jnp.where(high_y, implicit_diagonal, 0.0)

    square = (lax.broadcasted_iota(jnp.int32, (8, nz), 0) == lax.broadcasted_iota(jnp.int32, (8, nz), 1))

    def send_sums(step, sums):
        rows = [jnp.sum(m, axis=0, keepdims=True) for m in sums]
        rows = jnp.concatenate(rows + [jnp.zeros((8 - len(rows), nz), jnp.float32)], axis=0)
        totals = jnp.broadcast_to(jnp.sum(rows, axis=1, keepdims=True), (8, nz))
        slots[step, me] = jnp.sum(jnp.where(square, totals, 0.0), axis=0, keepdims=True)
        for off in range(1, count):
            to = {"gx": lax.rem(me_x + off // gy, gx), "gy": lax.rem(me_y + off % gy, gy)}
            pltpu.make_async_remote_copy(
                slots.at[step, me], slots.at[step, me], sum_send.at[step], sum_recv.at[step],
                device_id=to, device_id_type=MESH).start()

    def all_sums(step):
        some = slots.at[step, pl.ds(0, count - 1)]
        return pltpu.make_async_remote_copy(
            some, some, sum_send.at[step], sum_recv.at[step],
            device_id={"gx": lax.rem(me_x + 1, gx)}, device_id_type=MESH)

    def read_sums(step):
        all_sums(step).wait_recv()
        total = jnp.broadcast_to(jnp.sum(slots[step], axis=0), (8, nz))
        total = jnp.sum(jnp.where(square, total, 0.0), axis=1, keepdims=True)
        total = jnp.broadcast_to(total, (8, nz))
        return [total[k:k + 1] for k in range(4)]

    weights = []
    for step, section in enumerate((3, 2, 1)):
        r_tag, w_tag = 1 + step, 4 + step
        r_ref, w_ref = fields[r_tag], fields[w_tag]

        def first_pass(x, m0):
            if step == 0:
                c_ref = fields[0]
                r, more = section_weights[3] * (spread(c_ref, x)[1] + carried(c_ref, x)), None
            else:
                r, more = following(x)
            return m0 + fold(r * r), (r, more)

        def store_first(x, kept):
            r, more = kept
            keep(r_tag, x, r)
            yside[5, pl.ds(x, 1)] = r[1:2]
            if more is not None:
                fr[step - 1][x], dw[step - 1][x] = more

        outer = (0, 1, nx - 1)
        m0 = nothing
        if step == 0:
            with jax.named_scope("arrive0"):
                arrive(0, XD, XU, YD, YU)
                unpack(0)
            with jax.named_scope("first"):
                m0 = grouped("source", 2, nx - 1, first_pass, store_first, m0)
            with jax.named_scope("statics"):
                for xu, yu in statics:
                    pl.when(low_x)(xu.wait_recv)
                    pl.when(low_y)(yu.wait_recv)
                cx[0] = landed[0]
                mx[0] = landed[1]
                gdiag[0] += cx[0]
                fdiag[0] += mx[0]
                head = pl.ds(0, 1)
                for x in range(nx):
                    at = pl.ds(x, 1)
                    row = yrecv[7, 0, at]
                    cy[x, pl.ds(PAD - 1, 1)] = row
                    g = gdiag[x, head] + row
                    gdiag[x, head] = g
                    yside[3, at] = g
                    row = yrecv[8, 0, at]
                    my[x, pl.ds(PAD - 1, 1)] = row
                    fdiag[x, head] += row
                    yside[0, at] = cx[x + 1, head] if x < nx - 1 else jnp.zeros((1, nz), jnp.float32)
                    yside[4, at] = cx[x, head] if x else jnp.zeros((1, nz), jnp.float32)
                    yside[1, at] = cy[x, pl.ds(PAD, 1)]
                    yside[2, at] = czm[x, head]
            with jax.named_scope("firstedge"):
                for x in outer:
                    m0, kept = first_pass(x, m0)
                    store_first(x, kept)
                start(r_tag, XD, XU)
                inside = jnp.logical_and(row_x > 1, row_x < nx - 1)
                change = section_weights[3] * (yrecv[7, 0] + yrecv[8, 0]) * (yrecv[0, 0] - ysend[0, 0])
                change = jnp.where(inside, change, 0.0)
                r = ysend[r_tag, 0]
                m0 += fold((2.0 * r + change) * change)
                ysend[r_tag, 0] = r + change
                for x in range(2, nx - 1):
                    r_ref[1 + x, pl.ds(PAD, 1)] = ysend[r_tag, 0, pl.ds(x, 1)]
        else:
            with jax.named_scope("firstedge"):
                for x in outer:
                    m0, kept = first_pass(x, m0)
                    store_first(x, kept)
                start(r_tag, XD, XU)
        with jax.named_scope("corners"):
            w0 = inner(r_ref, 0)
            wpart[step] = w0
            w1 = inner(r_ref, nx - 1)
            corner = r_ref[1, pl.ds(PAD, 1)]
            corner_out[step, 0] = cy[0, pl.ds(PAD + ny - 1, 1)] * r_ref[1, pl.ds(PAD + ny - 1, 1)]
            corner_out[step, 1] = cy[0, pl.ds(PAD - 1, 1)] * corner
            corner_out[step, 2] = cx[0, pl.ds(0, 1)] * corner
            corner_out[step, 3] = cx[nx, pl.ds(0, 1)] * r_ref[nx, pl.ds(PAD, 1)]
            start(w_tag, XD)
        if step:
            with jax.named_scope("first"):
                m0 = grouped("next", 2, nx - 1, first_pass, store_first, m0)
        with jax.named_scope("ysend"):
            start(r_tag, YD, YU)
            for copy, toward, _ in corners(step):
                pl.when(toward)(copy.start)
            v = ysend[r_tag, 0]
            c = yside[2]
            total = yside[0] * pltpu.roll(v, nx - 1, 0) + yside[4] * pltpu.roll(v, 1, 0)
            total += yside[1] * yside[5] + c * ahead_z(v) + behind_z(c * v)
            ypart[step] = v - implicit_diagonal * (total - yside[3] * v)
            start(w_tag, YD)

        def second_pass(x, sums):
            m1, m2 = sums
            r, d = spread(r_ref, x)
            w = r - implicit_diagonal * d
            return (m1 + fold(r * w), m2 + fold(w * w)), w

        def store_second(x, w):
            keep(w_tag, x, w)

        with jax.named_scope("image"):
            sums = grouped("image", 1, nx - 1, second_pass, store_second, (nothing, nothing))

        def energy(x, low, rows):
            at, above = pl.ds(PAD + low, rows), pl.ds(PAD + low + 1, rows)
            mid = pl.ds(low, rows)
            w = w_ref[x + 1, at]
            jump_x = w_ref[x + 2, at] - w
            jump_y = w_ref[x + 1, above] - w
            jump_z = jnp.where(last_lane[:rows], 0.0, ahead_z(w)) - w
            total = cx[x + 1, mid] * jump_x * jump_x + cy[x, at] * jump_y * jump_y
            return fold(total + cz[x, mid] * jump_z * jump_z)

        with jax.named_scope("energy"):
            m3 = grouped("energy", 1, nx - 2, lambda x, m: (m + energy(x, 8, ny - 16), None), lambda x, kept: None, nothing)

        with jax.named_scope("arrive_y"):
            arrive(r_tag, YD, YU)
        with jax.named_scope("yfix"):
            unpack(r_tag)
            m1, m2 = sums
            for side, face in ((0, yrecv[7, 0]), (1, ysend[7, 1])):
                change = jnp.where(between, -implicit_diagonal * face * yrecv[r_tag, side], 0.0)
                w = ysend[w_tag, side]
                ysend[w_tag, side] = w + change
                m1 += fold(ysend[r_tag, side] * change)
                m2 += fold((2.0 * w + change) * change)
            for x in range(1, nx - 1):
                w_ref[1 + x, pl.ds(PAD, 1)] = ysend[w_tag, 0, pl.ds(x, 1)]
                w_ref[1 + x, pl.ds(PAD + ny - 1, 1)] = ysend[w_tag, 1, pl.ds(x, 1)]
        with jax.named_scope("rim"):
            m3 = grouped(
                "rim", 1, nx - 2, lambda x, m: (m + energy(x, 0, 8) + energy(x, ny - 8, 8), None), lambda x, kept: None, m3)
        with jax.named_scope("arrive_x"):
            arrive(r_tag, XD, XU)
        with jax.named_scope("edges"):
            sums = (m1, m2)
            for x in (0, nx - 1):
                sums, w = second_pass(x, sums)
                store_second(x, w)
            m1, m2 = sums
            start(w_tag, XU, YU)
        with jax.named_scope("arrive_w"):
            arrive(w_tag, XD, YD)
            for copy, _, whence in corners(step):
                pl.when(whence)(copy.wait_recv)
        with jax.named_scope("close"):
            w_ref[nx + 1, own] = w_ref[nx + 1, own] - across_x * (cx[nx] * r_ref[nx, own])
            for k, y in ((0, 0), (1, ny - 1)):
                w_ref[nx + 1, pl.ds(PAD + y, 1)] -= implicit_diagonal * corner_in[step, k]
            above = yrecv[w_tag, 1] - across_y * (ysend[7, 1] * ysend[r_tag, 1])
            above -= jnp.where(row_x == 0, implicit_diagonal * corner_in[step, 3], 0.0)
            above -= jnp.where(row_x == nx - 1, implicit_diagonal * corner_in[step, 2], 0.0)
            yrecv[w_tag, 1] = above
            for x in (0, nx - 2, nx - 1):
                m3 += energy(x, 0, ny)
            m3 += fold(ysend[7, 1] * above * (above - 2.0 * ysend[w_tag, 1]))
            m3 = m2 + implicit_diagonal * m3
        with jax.named_scope("sendsums"):
            send_sums(step, (m0, m1, m2, m3))

        def store_r(x, kept):
            fr[step][x] = kept

        with jax.named_scope("carry"):
            grouped("carry", 0, nx, lambda x, c: (c, carried(r_ref, x)), store_r, 0)

        target = section - 1
        share = section_weights[target] / section_weights[3]

        def gather(x, carry):
            total = share * fields[1][x + 1, own]
            for k in range(step):
                total += explicit_table[3 - k][target] * fr[k][x] + implicit_table[3 - k][target] * dw[k][x]
            if target == 0:
                total += fields[0][x + 1, own]
                for k in range(step):
                    on_r, on_w = weights[k]
                    total += on_r * fields[1 + k][x + 1, own] + on_w * fields[4 + k][x + 1, own]
            return carry, total

        def store_base(x, kept):
            base[x] = kept

        with jax.named_scope("gather"):
            grouped("gather", 0, nx, gather, store_base, 0)

        with jax.named_scope("arrive_up"):
            arrive(w_tag, XU, YU)
            unpack(w_tag)

        def store_w(x, kept):
            fw[step][x], dw[step][x] = kept

        with jax.named_scope("both"):
            grouped("both", 0, nx, lambda x, c: (c, (carried(w_ref, x), spread(w_ref, x)[1])), store_w, 0)

        with jax.named_scope("allsums"):
            m0, m1, m2, m3 = read_sums(step)
        alpha = m0 / m1
        rr = alpha * alpha * m2 - m0
        ratio = rr / m0
        product = m1 - 2.0 * alpha * m2 + alpha * alpha * m3
        alpha_next = rr / (product - ratio * rr / alpha)
        on_r = alpha + alpha_next * (1.0 + ratio)
        on_w = -alpha_next * alpha
        weights.append((on_r, on_w))

        def following(x, step=step, section=section, target=target, on_r=on_r, on_w=on_w):
            r, w = fields[1 + step][x + 1, own], fields[4 + step][x + 1, own]
            advected = on_r * fr[step][x] + on_w * fw[step][x]
            diffused = (on_r / implicit_diagonal) * (r - w) + on_w * dw[step][x]
            total = base[x]
            total += explicit_table[section][target] * advected
            total += implicit_table[section][target] * diffused
            if target == 0:
                return total + on_r * r + on_w * w
            return total, (advected, diffused)

    def last(x, carry):
        out_ref[x] = following(x)
        return carry

    with jax.named_scope("last"):
        lax.fori_loop(0, nx, last, 0)
    with jax.named_scope("sends"):
        for xu, yu in statics:
            pl.when(high_x)(xu.wait_send)
            pl.when(high_y)(yu.wait_send)
        for tag in range(7):
            sent(tag)
        for step in range(3):
            for copy, toward, _ in corners(step):
                pl.when(toward)(copy.wait_send)
            all_sums(step).wait_send()


def local(gx, gy, cotangent, speed, coeff, dirs):
    nx, ny, nz = cotangent.shape
    f32 = jnp.float32
    rows = ny + 2 * PAD
    plain = pltpu.VMEM((nx, ny, nz), f32)
    dma = pltpu.SemaphoreType.DMA
    far = pl.BlockSpec(memory_space=pltpu.HBM)
    hbm = [pltpu.with_memory_space_constraint(v, pltpu.HBM) for v in (cotangent, speed, coeff)]
    return pl.pallas_call(
        functools.partial(kernel, gx, gy),
        out_shape=jax.ShapeDtypeStruct((nx, ny, nz), f32),
        in_specs=[far, far, far, pl.BlockSpec(memory_space=pltpu.VMEM)],
        out_specs=pl.BlockSpec(memory_space=pltpu.VMEM),
        scratch_shapes=[
            *[pltpu.VMEM((nx + 2, rows, nz), f32)] * 7,
            *[plain] * 9,
            plain,
            pltpu.VMEM((nx + 1, ny, nz), f32),
            pltpu.VMEM((nx, rows, nz), f32),
            plain, plain,
            plain, plain, plain,
            pltpu.VMEM((nx + 1, ny, nz), f32),
            pltpu.VMEM((nx, rows, nz), f32),
            plain,
            plain, plain,
            pltpu.VMEM((9, 2, nx, nz), f32),
            pltpu.VMEM((9, 2, nx, nz), f32),
            pltpu.VMEM((2, ny, nz), f32),
            pltpu.VMEM((3, ny, nz), f32),
            pltpu.VMEM((3, nx, nz), f32),
            pltpu.VMEM((6, nx, nz), f32),
            pltpu.VMEM((3, 4, 1, nz), f32),
            pltpu.VMEM((3, 4, 1, nz), f32),
            pltpu.VMEM((3, gx * gy, 1, nz), f32),
            dma((1 + 6 * CHUNKS,)), dma((9, 4)), dma((9, 4)),
            dma((3, 3)), dma((3, 3)), dma((3,)), dma((3,)),
        ],
        compiler_params=pltpu.CompilerParams(
            collective_id=0, has_side_effects=True, vmem_limit_bytes=46 * 1024 * 1024
        ),
    )(*hbm, dirs)


def solution(mesh):
    return jax.shard_map(
        functools.partial(local, mesh.shape["gx"], mesh.shape["gy"]),
        mesh=mesh,
        in_specs=(
            P("gx", "gy", None),
            P(None, "gx", "gy", None),
            P(None, "gx", "gy", None),
            P(None, "gx", "gy"),
        ),
        out_specs=P("gx", "gy", None),
        check_vma=False,
    )
```

time: 60.4 us -> 44.6 us (0.74)
  Pallas kernels: 57.9 us -> 42.6 us
    pallas_call x1, Pallas kernels: 57.9 us -> 42.6 us  [local(): pl.pallas_call(functools.partial(kernel, gx, gy), out_shape=jax.ShapeDtyp...]
    unnamed x1 -> x3, local copies, waits for them, and re-layouts: 2.31 us -> 1.77 us
where the time goes in v1:
time: 44.6 us; the launch traced here: 44.4 us
  Pallas kernels  42.6 us (96%)
  local copies, waits for them, and re-layouts  1.77 us (4%)
    pallas_call x1, Pallas kernels, local(): pl.pallas_call(functools.partial(kernel, gx, gy), out_shape=jax.ShapeDtyp...  42.6 us
    unnamed x3, local copies, waits for them, and re-layouts  1.77 us

profile of v1, /device:TPU:0, one launch (start us, length us, event | category | flops | bytes accessed | tf_op | source)
XLA Modules:
  0.0 44.4 jit_solution(2179953295271341966)
XLA Ops:
  0.0 0.0 copy-start
  0.0 0.8 %copy-done = s32[3,32,64]{2,1,0:T(8,128)S(1)} copy-done((s32[3,32,64]{2,1,0:T(8,128)S(1)}, s32[3,32,64]{2,1,0:T(8,128)}, u32[]{:S(2)}) %copy-start) | copy-done | bytes 24600
  0.8 42.6 %shard_map.46 = f32[32,64,128]{2,1,0:T(8,128)S(1)} custom-call(f32[32,64,128]{2,1,0:T(8,128)} %cot_hbm.1, f32[3,32,64,128]{3,2,1,0:T(8,128)} %speed_hbm.1, f32[3,32,64,128]{3,2,1,0:T(8,128)} %coeff_hbm.1, s32[3,32,64]{2,1,0:T(8,128)S(1)} %copy-done), custom_call_target="tpu_custom_call" | custom-call | tf_op jit(solution)/shard_map/pallas_call | solution.py:563
  43.4 1.0 %copy.6 = f32[32,64,128]{2,1,0:T(8,128)} copy(f32[32,64,128]{2,1,0:T(8,128)S(1)} %shard_map.46) | data formatting | bytes 2097152
Async XLA Ops:
  0.0 0.8 %copy-start = (s32[3,32,64]{2,1,0:T(8,128)S(1)}, s32[3,32,64]{2,1,0:T(8,128)}, u32[]{:S(2)}) copy-start(s32[3,32,64]{2,1,0:T(8,128)} %dirs_ref.1) | copy-start | bytes 73732

commit v2 on v1

--- a/solution.py
+++ b/solution.py
@@ -26,7 +26,7 @@
 PAD = 8
 
 
-GROUP = {"masks": 4, "diagonals": 2, "source": 2, "next": 2, "image": 2, "energy": 4, "rim": 4, "carry": 4, "both": 2, "gather": 2}
+GROUP = {"masks": 8, "diagonals": 8, "source": 15, "strip": 29, "next": 29, "image": 10, "energy": 14, "rim": 28, "carry": 16, "both": 8, "gather": 16, "last": 8}
 CHUNKS = 4
 
 
@@ -50,9 +50,9 @@
 
 
 def kernel(
-    gx, gy, cot_hbm, speed_hbm, coeff_hbm, dirs_ref, out_ref,
+    gx, gy, cot_hbm, speed_hbm, coeff_hbm, dirs_hbm, out_ref,
     f0, f1, f2, f3, f4, f5, f6, fr0, fr1, fr2, fw0, fw1, fw2, dw0, dw1, dw2, base, cx, cy, cz, czm, px, py, pz, mx, my, mz, gdiag, fdiag,
-    ysend, yrecv, landed, wpart, ypart, yside, corner_out, corner_in, slots,
+    ysend, yrecv, dirs_ref, landed, wpart, ypart, yside, corner_out, corner_in, slots,
     load_sem, send_sem, recv_sem, corner_send, corner_recv, sum_send, sum_recv,
 ):
     nx, ny, nz = out_ref.shape
@@ -85,6 +85,7 @@
 
     with jax.named_scope("loads"):
         cot_load = load(0, cot_hbm, fields[0].at[pl.ds(1, nx), own])
+        dirs_load = load(1 + 6 * chunks, dirs_hbm, dirs_ref)
         loads = []
         for chunk in range(chunks):
             at = pl.ds(chunk * piece, piece)
@@ -163,6 +164,11 @@
         for k in which:
             pl.when(starts[k])(every[k].start)
 
+    odd = lax.rem(me_x, 2) == 1
+
+    def start_if(also, tag, k):
+        pl.when(jnp.logical_and(also, starts[k]))(copies(tag)[k].start)
+
     def arrive(tag, *which):
         every = copies(tag)
         for k in which:
@@ -193,6 +199,7 @@
 
     with jax.named_scope("barrier"):
         cot_load.wait()
+        dirs_load.wait()
         for x in range(nx):
             at = pl.ds(x, 1)
             ysend[0, 0, at] = fields[0][x + 1, pl.ds(PAD, 1)]
@@ -321,16 +328,45 @@
             if step == 0:
                 c_ref = fields[0]
                 r, more = section_weights[3] * (spread(c_ref, x)[1] + carried(c_ref, x)), None
-            else:
-                r, more = following(x)
             return m0 + fold(r * r), (r, more)
 
         def store_first(x, kept):
             r, more = kept
             keep(r_tag, x, r)
             yside[5, pl.ds(x, 1)] = r[1:2]
-            if more is not None:
-                fr[step - 1][x], dw[step - 1][x] = more
+
+        def part(low, rows):
+            at, mid = pl.ds(PAD + low, rows), pl.ds(low, rows)
+
+            def value(x, m0):
+                r, more = following(x, low, rows)
+                return m0 + fold(r * r), (r, more)
+
+            def store(x, kept):
+                r, more = kept
+                r_ref[x + 1, at] = r
+                if low < 8:
+                    ysend[r_tag, 0, pl.ds(x, 1)] = r[:1]
+                    yside[5, pl.ds(x, 1)] = r[1:2]
+                if low + rows == ny:
+                    ysend[r_tag, 1, pl.ds(x, 1)] = r[rows - 1:]
+                fr[step - 1][x, mid], dw[step - 1][x, mid] = more
+
+            return value, store
+
+        def send_x():
+            corner = r_ref[1, pl.ds(PAD, 1)]
+            corner_out[step, 0] = cy[0, pl.ds(PAD + ny - 1, 1)] * r_ref[1, pl.ds(PAD + ny - 1, 1)]
+            corner_out[step, 1] = cy[0, pl.ds(PAD - 1, 1)] * corner
+            corner_out[step, 2] = cx[0, pl.ds(0, 1)] * corner
+            corner_out[step, 3] = cx[nx, pl.ds(0, 1)] * r_ref[nx, pl.ds(PAD, 1)]
+            for copy, toward, _ in corners(step):
+                pl.when(toward)(copy.start)
+            start_if(True, r_tag, XD)
+            start_if(odd, r_tag, XU)
+            wpart[step] = inner(r_ref, 0)
+            start_if(jnp.logical_not(odd), w_tag, XD)
+            start_if(jnp.logical_not(odd), r_tag, XU)
 
         outer = (0, 1, nx - 1)
         m0 = nothing
@@ -367,7 +403,6 @@
                 for x in outer:
                     m0, kept = first_pass(x, m0)
                     store_first(x, kept)
-                start(r_tag, XD, XU)
                 inside = jnp.logical_and(row_x > 1, row_x < nx - 1)
                 change = section_weights[3] * (yrecv[7, 0] + yrecv[8, 0]) * (yrecv[0, 0] - ysend[0, 0])
                 change = jnp.where(inside, change, 0.0)
@@ -376,35 +411,32 @@
                 ysend[r_tag, 0] = r + change
                 for x in range(2, nx - 1):
                     r_ref[1 + x, pl.ds(PAD, 1)] = ysend[r_tag, 0, pl.ds(x, 1)]
+                send_x()
+                start(r_tag, YD, YU)
         else:
             with jax.named_scope("firstedge"):
+                value, store = part(0, ny)
                 for x in outer:
-                    m0, kept = first_pass(x, m0)
-                    store_first(x, kept)
-                start(r_tag, XD, XU)
+                    m0, kept = value(x, m0)
+                    store(x, kept)
+                send_x()
+            with jax.named_scope("strips"):
+                for low in (0, ny - 8):
+                    value, store = part(low, 8)
+                    m0 = grouped("strip", 2, nx - 1, value, store, m0)
+                start(r_tag, YD, YU)
         with jax.named_scope("corners"):
-            w0 = inner(r_ref, 0)
-            wpart[step] = w0
-            w1 = inner(r_ref, nx - 1)
-            corner = r_ref[1, pl.ds(PAD, 1)]
-            corner_out[step, 0] = cy[0, pl.ds(PAD + ny - 1, 1)] * r_ref[1, pl.ds(PAD + ny - 1, 1)]
-            corner_out[step, 1] = cy[0, pl.ds(PAD - 1, 1)] * corner
-            corner_out[step, 2] = cx[0, pl.ds(0, 1)] * corner
-            corner_out[step, 3] = cx[nx, pl.ds(0, 1)] * r_ref[nx, pl.ds(PAD, 1)]
-            start(w_tag, XD)
-        if step:
-            with jax.named_scope("first"):
-                m0 = grouped("next", 2, nx - 1, first_pass, store_first, m0)
-        with jax.named_scope("ysend"):
-            start(r_tag, YD, YU)
-            for copy, toward, _ in corners(step):
-                pl.when(toward)(copy.start)
             v = ysend[r_tag, 0]
             c = yside[2]
             total = yside[0] * pltpu.roll(v, nx - 1, 0) + yside[4] * pltpu.roll(v, 1, 0)
             total += yside[1] * yside[5] + c * ahead_z(v) + behind_z(c * v)
             ypart[step] = v - implicit_diagonal * (total - yside[3] * v)
             start(w_tag, YD)
+            start_if(odd, w_tag, XD)
+        if step:
+            value, store = part(8, ny - 16)
+            with jax.named_scope("first"):
+                m0 = grouped("next", 2, nx - 1, value, store, m0)
 
         def second_pass(x, sums):
             m1, m2 = sums
@@ -456,7 +488,6 @@
                 sums, w = second_pass(x, sums)
                 store_second(x, w)
             m1, m2 = sums
-            start(w_tag, XU, YU)
         with jax.named_scope("arrive_w"):
             arrive(w_tag, XD, YD)
             for copy, _, whence in corners(step):
@@ -475,6 +506,7 @@
             m3 = m2 + implicit_diagonal * m3
         with jax.named_scope("sendsums"):
             send_sums(step, (m0, m1, m2, m3))
+            start(w_tag, YU, XU)
 
         def store_r(x, kept):
             fr[step][x] = kept
@@ -523,23 +555,23 @@
         on_w = -alpha_next * alpha
         weights.append((on_r, on_w))
 
-        def following(x, step=step, section=section, target=target, on_r=on_r, on_w=on_w):
-            r, w = fields[1 + step][x + 1, own], fields[4 + step][x + 1, own]
-            advected = on_r * fr[step][x] + on_w * fw[step][x]
-            diffused = (on_r / implicit_diagonal) * (r - w) + on_w * dw[step][x]
-            total = base[x]
+        def following(x, low=0, rows=ny, step=step, section=section, target=target, on_r=on_r, on_w=on_w):
+            at, mid = pl.ds(PAD + low, rows), pl.ds(low, rows)
+            r, w = fields[1 + step][x + 1, at], fields[4 + step][x + 1, at]
+            advected = on_r * fr[step][x, mid] + on_w * fw[step][x, mid]
+            diffused = (on_r / implicit_diagonal) * (r - w) + on_w * dw[step][x, mid]
+            total = base[x, mid]
             total += explicit_table[section][target] * advected
             total += implicit_table[section][target] * diffused
             if target == 0:
                 return total + on_r * r + on_w * w
             return total, (advected, diffused)
 
-    def last(x, carry):
-        out_ref[x] = following(x)
-        return carry
+    def store_out(x, kept):
+        out_ref[x] = kept
 
     with jax.named_scope("last"):
-        lax.fori_loop(0, nx, last, 0)
+        grouped("last", 0, nx, lambda x, c: (c, following(x)), store_out, 0)
     with jax.named_scope("sends"):
         for xu, yu in statics:
             pl.when(high_x)(xu.wait_send)
@@ -559,11 +591,11 @@
     plain = pltpu.VMEM((nx, ny, nz), f32)
     dma = pltpu.SemaphoreType.DMA
     far = pl.BlockSpec(memory_space=pltpu.HBM)
-    hbm = [pltpu.with_memory_space_constraint(v, pltpu.HBM) for v in (cotangent, speed, coeff)]
+    hbm = [pltpu.with_memory_space_constraint(v, pltpu.HBM) for v in (cotangent, speed, coeff, dirs)]
     return pl.pallas_call(
         functools.partial(kernel, gx, gy),
         out_shape=jax.ShapeDtypeStruct((nx, ny, nz), f32),
-        in_specs=[far, far, far, pl.BlockSpec(memory_space=pltpu.VMEM)],
+        in_specs=[far] * 4,
         out_specs=pl.BlockSpec(memory_space=pltpu.VMEM),
         scratch_shapes=[
             *[pltpu.VMEM((nx + 2, rows, nz), f32)] * 7,
@@ -579,6 +611,7 @@
             plain, plain,
             pltpu.VMEM((9, 2, nx, nz), f32),
             pltpu.VMEM((9, 2, nx, nz), f32),
+            pltpu.VMEM(dirs.shape, dirs.dtype),
             pltpu.VMEM((2, ny, nz), f32),
             pltpu.VMEM((3, ny, nz), f32),
             pltpu.VMEM((3, nx, nz), f32),
@@ -586,13 +619,13 @@
             pltpu.VMEM((3, 4, 1, nz), f32),
             pltpu.VMEM((3, 4, 1, nz), f32),
             pltpu.VMEM((3, gx * gy, 1, nz), f32),
-            dma((1 + 6 * CHUNKS,)), dma((9, 4)), dma((9, 4)),
+            dma((2 + 6 * CHUNKS,)), dma((9, 4)), dma((9, 4)),
             dma((3, 3)), dma((3, 3)), dma((3,)), dma((3,)),
         ],
         compiler_params=pltpu.CompilerParams(
             collective_id=0, has_side_effects=True, vmem_limit_bytes=46 * 1024 * 1024
         ),
-    )(*hbm, dirs)
+    )(*hbm)
 
 
 def solution(mesh):

time: 44.6 us -> 41.2 us (0.924)
  Pallas kernels: 42.6 us -> 40.1 us
  local copies, waits for them, and re-layouts: 1.77 us -> 0.97 us
    pallas_call x1, Pallas kernels: 42.6 us -> 40.1 us  [local(): pl.pallas_call(functools.partial(kernel, gx, gy), out_shape=jax.ShapeDtyp...]
    unnamed x3 -> x1, local copies, waits for them, and re-layouts: 1.77 us -> 0.97 us
where the time goes in v2:
time: 41.2 us; the launch traced here: 41.1 us
  Pallas kernels  40.1 us (97%)
  local copies, waits for them, and re-layouts  0.97 us (2%)
    pallas_call x1, Pallas kernels, local(): pl.pallas_call(functools.partial(kernel, gx, gy), out_shape=jax.ShapeDtyp...  40.1 us
    unnamed x1, local copies, waits for them, and re-layouts  0.97 us

profile of v2, /device:TPU:0, one launch (start us, length us, event | category | flops | bytes accessed | tf_op | source)
XLA Modules:
  0.0 41.1 jit_solution(17998005040308537836)
XLA Ops:
  0.0 40.1 %shard_map.46 = f32[32,64,128]{2,1,0:T(8,128)S(1)} custom-call(f32[32,64,128]{2,1,0:T(8,128)} %cot_hbm.1, f32[3,32,64,128]{3,2,1,0:T(8,128)} %speed_hbm.1, f32[3,32,64,128]{3,2,1,0:T(8,128)} %coeff_hbm.1, s32[3,32,64]{2,1,0:T(8,128)} %dirs_hbm.1), custom_call_target="tpu_custom_call" | custom-call | tf_op jit(solution)/shard_map/pallas_call | solution.py:595
  40.1 1.0 %copy.6 = f32[32,64,128]{2,1,0:T(8,128)} copy(f32[32,64,128]{2,1,0:T(8,128)S(1)} %shard_map.46) | data formatting | bytes 2097152

commit v3 on v2

--- a/solution.py
+++ b/solution.py
@@ -50,14 +50,14 @@
 
 
 def kernel(
-    gx, gy, cot_hbm, speed_hbm, coeff_hbm, dirs_hbm, out_ref,
-    f0, f1, f2, f3, f4, f5, f6, fr0, fr1, fr2, fw0, fw1, fw2, dw0, dw1, dw2, base, cx, cy, cz, czm, px, py, pz, mx, my, mz, gdiag, fdiag,
-    ysend, yrecv, dirs_ref, landed, wpart, ypart, yside, corner_out, corner_in, slots,
+    gx, gy, cot_hbm, speed_hbm, coeff_hbm, dirs_hbm, out_base, out_r, out_w, out_scale,
+    f0, f1, f2, f3, f4, f5, f6, fr0, fr1, fw0, fw1, dw0, dw1, base, cx, cy, cz, czm, px, py, pz, mx, my, mz, gdiag, fdiag,
+    ysend, yrecv, dirs_ref, cx_top, mx_top, cy_top, py_top, landed, wpart, ypart, yside, corner_out, corner_in, slots,
     load_sem, send_sem, recv_sem, corner_send, corner_recv, sum_send, sum_recv,
 ):
-    nx, ny, nz = out_ref.shape
+    nx, ny, nz = out_base.shape
     fields = (f0, f1, f2, f3, f4, f5, f6)
-    fr, fw, dw = (fr0, fr1, fr2), (fw0, fw1, fw2), (dw0, dw1, dw2)
+    fr, fw, dw = (fr0, fr1), (fw0, fw1), (dw0, dw1)
     me_x, me_y = lax.axis_index("gx"), lax.axis_index("gy")
     count = gx * gy
     me = me_x * gy + me_y
@@ -84,6 +84,13 @@
         return copy
 
     with jax.named_scope("loads"):
+        first = 2 + 6 * chunks
+        tops = [
+            load(first, coeff_hbm.at[0, nx - 1], cx_top),
+            load(first + 1, speed_hbm.at[0, nx - 1], mx_top),
+            load(first + 2, coeff_hbm.at[1, :, pl.ds(ny - 8, 8)], cy_top),
+            load(first + 3, speed_hbm.at[1, :, pl.ds(ny - 8, 8)], py_top),
+        ]
         cot_load = load(0, cot_hbm, fields[0].at[pl.ds(1, nx), own])
         dirs_load = load(1 + 6 * chunks, dirs_hbm, dirs_ref)
         loads = []
@@ -121,7 +128,7 @@
         def zero_rows(x, carry):
             cy[x, pl.ds(0, PAD)] = jnp.zeros((PAD, nz), jnp.float32)
             my[x, pl.ds(0, PAD)] = jnp.zeros((PAD, nz), jnp.float32)
-            for k in range(1, 7):
+            for k in range(7):
                 fields[k][x + 1, pl.ds(0, PAD)] = jnp.zeros((PAD, nz), jnp.float32)
                 fields[k][x + 1, pl.ds(PAD + ny, PAD)] = jnp.zeros((PAD, nz), jnp.float32)
             return carry
@@ -205,12 +212,30 @@
             ysend[0, 0, at] = fields[0][x + 1, pl.ds(PAD, 1)]
             ysend[0, 1, at] = fields[0][x + 1, pl.ds(PAD + ny - 1, 1)]
         dirs = [dirs_ref[d].astype(jnp.float32).T for d in range(3)]
+
+        def upper(d, x):
+            column = (lax.broadcasted_iota(jnp.int32, (nx, nz), 0) == x).astype(jnp.float32)
+            return jnp.dot(dirs[d], column, preferred_element_type=jnp.float32) > 0.5
+
+        for copy in tops:
+            copy.wait()
+        mx_top[...] = jnp.where(upper(0, nx - 1), mx_top[...], 0.0)
+        for x in range(nx):
+            at = pl.ds(x, 1)
+            ysend[7, 1, at] = cy_top[x, 7:]
+            yside[6, at] = py_top[x, 7:]
+        edge = jnp.broadcast_to(dirs_ref[1][:, ny - 1:], (nx, nz)) > 0
+        ysend[8, 1] = jnp.where(edge, yside[6], 0.0)
+        yside[6] = jnp.where(edge, 0.0, yside[6])
         pl.semaphore_wait(barrier, count - 1)
-    start(0, XD, XU, YD, YU)
-
-    def upper(d, x):
-        column = (lax.broadcasted_iota(jnp.int32, (nx, nz), 0) == x).astype(jnp.float32)
-        return jnp.dot(dirs[d], column, preferred_element_type=jnp.float32) > 0.5
+        start(0, YD, YU, XD, XU)
+        statics = (
+            (x_up(7, cx_top, landed.at[0]), y_up(7)),
+            (x_up(8, mx_top, landed.at[1]), y_up(8)),
+        )
+        for xu, yu in statics:
+            pl.when(high_x)(xu.start)
+            pl.when(high_y)(yu.start)
 
     def masks(x, carry):
         low = [jnp.where(upper(d, x), ref[x], 0.0) for d, ref in enumerate((px, py, pz))]
@@ -218,15 +243,12 @@
 
     def store_masks(x, kept):
         low, high, c = kept
-        at = pl.ds(x, 1)
         mx[x + 1] = low[0]
         my[x, own] = low[1]
         mz[x] = jnp.where(last_lane, 0.0, low[2])
         px[x], py[x] = high[0], high[1]
         pz[x] = high[2]
         czm[x] = jnp.where(last_lane, 0.0, c)
-        ysend[8, 1, at] = low[1][ny - 1:]
-        ysend[7, 1, at] = cy[x, pl.ds(PAD + ny - 1, 1)]
 
     def diagonals(x, carry):
         p = pz[x]
@@ -246,14 +268,6 @@
             grouped("masks", low, high, masks, store_masks, 0)
         with jax.named_scope("diagonals"):
             grouped("diagonals", low, high, diagonals, store_diagonals, 0)
-
-    statics = (
-        (x_up(7, cx.at[nx], landed.at[0]), y_up(7)),
-        (x_up(8, mx.at[nx], landed.at[1]), y_up(8)),
-    )
-    for xu, yu in statics:
-        pl.when(high_x)(xu.start)
-        pl.when(high_y)(yu.start)
 
     def spread(ref, x):
         v = ref[x + 1, own]
@@ -371,11 +385,13 @@
         outer = (0, 1, nx - 1)
         m0 = nothing
         if step == 0:
+            with jax.named_scope("first"):
+                m0 = grouped("source", 2, nx - 1, first_pass, store_first, m0)
             with jax.named_scope("arrive0"):
                 arrive(0, XD, XU, YD, YU)
-                unpack(0)
-            with jax.named_scope("first"):
-                m0 = grouped("source", 2, nx - 1, first_pass, store_first, m0)
+                for x in outer:
+                    fields[0][1 + x, pl.ds(PAD - 1, 1)] = yrecv[0, 0, pl.ds(x, 1)]
+                    fields[0][1 + x, pl.ds(PAD + ny, 1)] = yrecv[0, 1, pl.ds(x, 1)]
             with jax.named_scope("statics"):
                 for xu, yu in statics:
                     pl.when(low_x)(xu.wait_recv)
@@ -403,15 +419,20 @@
                 for x in outer:
                     m0, kept = first_pass(x, m0)
                     store_first(x, kept)
+                send_x()
+            with jax.named_scope("patch"):
                 inside = jnp.logical_and(row_x > 1, row_x < nx - 1)
-                change = section_weights[3] * (yrecv[7, 0] + yrecv[8, 0]) * (yrecv[0, 0] - ysend[0, 0])
-                change = jnp.where(inside, change, 0.0)
-                r = ysend[r_tag, 0]
-                m0 += fold((2.0 * r + change) * change)
-                ysend[r_tag, 0] = r + change
+                for side, change in (
+                    (0, (yrecv[7, 0] + yrecv[8, 0]) * (yrecv[0, 0] - ysend[0, 0])),
+                    (1, (ysend[7, 1] + yside[6]) * yrecv[0, 1]),
+                ):
+                    change = jnp.where(inside, section_weights[3] * change, 0.0)
+                    r = ysend[r_tag, side]
+                    m0 += fold((2.0 * r + change) * change)
+                    ysend[r_tag, side] = r + change
                 for x in range(2, nx - 1):
                     r_ref[1 + x, pl.ds(PAD, 1)] = ysend[r_tag, 0, pl.ds(x, 1)]
-                send_x()
+                    r_ref[1 + x, pl.ds(PAD + ny - 1, 1)] = ysend[r_tag, 1, pl.ds(x, 1)]
                 start(r_tag, YD, YU)
         else:
             with jax.named_scope("firstedge"):
@@ -499,7 +520,6 @@
             above = yrecv[w_tag, 1] - across_y * (ysend[7, 1] * ysend[r_tag, 1])
             above -= jnp.where(row_x == 0, implicit_diagonal * corner_in[step, 3], 0.0)
             above -= jnp.where(row_x == nx - 1, implicit_diagonal * corner_in[step, 2], 0.0)
-            yrecv[w_tag, 1] = above
             for x in (0, nx - 2, nx - 1):
                 m3 += energy(x, 0, ny)
             m3 += fold(ysend[7, 1] * above * (above - 2.0 * ysend[w_tag, 1]))
@@ -507,17 +527,29 @@
         with jax.named_scope("sendsums"):
             send_sums(step, (m0, m1, m2, m3))
             start(w_tag, YU, XU)
+            for x in range(nx):
+                w_ref[1 + x, pl.ds(PAD + ny, 1)] = above[x:x + 1]
+
+        target = section - 1
+        final = target == 0
+        on_f, on_d = explicit_table[section][target], implicit_table[section][target]
+
+        def carry(x, c):
+            f = carried(r_ref, x)
+            if final:
+                r = r_ref[x + 1, own]
+                f = on_f * f + ((on_d / implicit_diagonal) * (r - w_ref[x + 1, own]) + r)
+            return c, f
 
         def store_r(x, kept):
-            fr[step][x] = kept
+            (out_r if final else fr[step])[x] = kept
 
         with jax.named_scope("carry"):
-            grouped("carry", 0, nx, lambda x, c: (c, carried(r_ref, x)), store_r, 0)
-
-        target = section - 1
+            grouped("carry", 0, nx, carry, store_r, 0)
+
         share = section_weights[target] / section_weights[3]
 
-        def gather(x, carry):
+        def gather(x, c):
             total = share * fields[1][x + 1, own]
             for k in range(step):
                 total += explicit_table[3 - k][target] * fr[k][x] + implicit_table[3 - k][target] * dw[k][x]
@@ -526,23 +558,41 @@
                 for k in range(step):
                     on_r, on_w = weights[k]
                     total += on_r * fields[1 + k][x + 1, own] + on_w * fields[4 + k][x + 1, own]
-            return carry, total
+            return c, total
 
         def store_base(x, kept):
-            base[x] = kept
+            (out_base if final else base)[x] = kept
 
         with jax.named_scope("gather"):
             grouped("gather", 0, nx, gather, store_base, 0)
 
+        def store_w(x, kept):
+            if final:
+                out_w[x] = kept
+            else:
+                fw[step][x], dw[step][x] = kept
+
+        def both(x, c):
+            f, (w, d) = carried(w_ref, x), spread(w_ref, x)
+            return c, on_f * f + on_d * d + w if final else (f, d)
+
+        with jax.named_scope("both"):
+            grouped("both", 1, nx, both, store_w, 0)
         with jax.named_scope("arrive_up"):
             arrive(w_tag, XU, YU)
-            unpack(w_tag)
-
-        def store_w(x, kept):
-            fw[step][x], dw[step][x] = kept
-
-        with jax.named_scope("both"):
-            grouped("both", 0, nx, lambda x, c: (c, (carried(w_ref, x), spread(w_ref, x)[1])), store_w, 0)
+        with jax.named_scope("late"):
+            w_ref[1, pl.ds(PAD - 1, 1)] = yrecv[w_tag, 0, pl.ds(0, 1)]
+            store_w(0, both(0, 0)[1])
+            head = pl.ds(0, 1)
+            owed_f = yrecv[8, 0] * yrecv[w_tag, 0]
+            owed_d = yrecv[7, 0] * yrecv[w_tag, 0]
+            owed = on_f * owed_f + on_d * owed_d
+            for x in range(1, nx):
+                if final:
+                    out_w[x, head] += owed[x:x + 1]
+                else:
+                    fw[step][x, head] += owed_f[x:x + 1]
+                    dw[step][x, head] += owed_d[x:x + 1]
 
         with jax.named_scope("allsums"):
             m0, m1, m2, m3 = read_sums(step)
@@ -555,23 +605,16 @@
         on_w = -alpha_next * alpha
         weights.append((on_r, on_w))
 
-        def following(x, low=0, rows=ny, step=step, section=section, target=target, on_r=on_r, on_w=on_w):
+        def following(x, low, rows, step=step, on_r=on_r, on_w=on_w, on_f=on_f, on_d=on_d):
             at, mid = pl.ds(PAD + low, rows), pl.ds(low, rows)
             r, w = fields[1 + step][x + 1, at], fields[4 + step][x + 1, at]
             advected = on_r * fr[step][x, mid] + on_w * fw[step][x, mid]
             diffused = (on_r / implicit_diagonal) * (r - w) + on_w * dw[step][x, mid]
             total = base[x, mid]
-            total += explicit_table[section][target] * advected
-            total += implicit_table[section][target] * diffused
-            if target == 0:
-                return total + on_r * r + on_w * w
+            total += on_f * advected + on_d * diffused
             return total, (advected, diffused)
 
-    def store_out(x, kept):
-        out_ref[x] = kept
-
-    with jax.named_scope("last"):
-        grouped("last", 0, nx, lambda x, c: (c, following(x)), store_out, 0)
+    out_scale[...] = jnp.concatenate(weights[-1], axis=0)
     with jax.named_scope("sends"):
         for xu, yu in statics:
             pl.when(high_x)(xu.wait_send)
@@ -584,6 +627,21 @@
             all_sums(step).wait_send()
 
 
+def finish(base, on_r, on_w, scale, out_hbm, out, sem):
+    nx = base.shape[0]
+    chunks = CHUNKS if nx % CHUNKS == 0 else 1
+    piece = nx // chunks
+    copies = []
+    for chunk in range(chunks):
+        at = pl.ds(chunk * piece, piece)
+        for x in range(chunk * piece, (chunk + 1) * piece):
+            out[x] = base[x] + scale[:1] * on_r[x] + scale[1:] * on_w[x]
+        copies.append(pltpu.make_async_copy(out.at[at], out_hbm.at[at], sem.at[chunk]))
+        copies[-1].start()
+    for copy in copies:
+        copy.wait()
+
+
 def local(gx, gy, cotangent, speed, coeff, dirs):
     nx, ny, nz = cotangent.shape
     f32 = jnp.float32
@@ -592,14 +650,15 @@
     dma = pltpu.SemaphoreType.DMA
     far = pl.BlockSpec(memory_space=pltpu.HBM)
     hbm = [pltpu.with_memory_space_constraint(v, pltpu.HBM) for v in (cotangent, speed, coeff, dirs)]
-    return pl.pallas_call(
+    whole = jax.ShapeDtypeStruct((nx, ny, nz), f32)
+    total, on_r, on_w, scale = pl.pallas_call(
         functools.partial(kernel, gx, gy),
-        out_shape=jax.ShapeDtypeStruct((nx, ny, nz), f32),
+        out_shape=(whole, whole, whole, jax.ShapeDtypeStruct((2, nz), f32)),
         in_specs=[far] * 4,
-        out_specs=pl.BlockSpec(memory_space=pltpu.VMEM),
+        out_specs=(pl.BlockSpec(memory_space=pltpu.VMEM),) * 4,
         scratch_shapes=[
             *[pltpu.VMEM((nx + 2, rows, nz), f32)] * 7,
-            *[plain] * 9,
+            *[plain] * 6,
             plain,
             pltpu.VMEM((nx + 1, ny, nz), f32),
             pltpu.VMEM((nx, rows, nz), f32),
@@ -612,20 +671,32 @@
             pltpu.VMEM((9, 2, nx, nz), f32),
             pltpu.VMEM((9, 2, nx, nz), f32),
             pltpu.VMEM(dirs.shape, dirs.dtype),
+            pltpu.VMEM((ny, nz), f32),
+            pltpu.VMEM((ny, nz), f32),
+            pltpu.VMEM((nx, 8, nz), f32),
+            pltpu.VMEM((nx, 8, nz), f32),
             pltpu.VMEM((2, ny, nz), f32),
             pltpu.VMEM((3, ny, nz), f32),
             pltpu.VMEM((3, nx, nz), f32),
-            pltpu.VMEM((6, nx, nz), f32),
+            pltpu.VMEM((7, nx, nz), f32),
             pltpu.VMEM((3, 4, 1, nz), f32),
             pltpu.VMEM((3, 4, 1, nz), f32),
             pltpu.VMEM((3, gx * gy, 1, nz), f32),
-            dma((2 + 6 * CHUNKS,)), dma((9, 4)), dma((9, 4)),
+            dma((6 + 6 * CHUNKS,)), dma((9, 4)), dma((9, 4)),
             dma((3, 3)), dma((3, 3)), dma((3,)), dma((3,)),
         ],
         compiler_params=pltpu.CompilerParams(
             collective_id=0, has_side_effects=True, vmem_limit_bytes=46 * 1024 * 1024
         ),
     )(*hbm)
+    return pl.pallas_call(
+        finish,
+        out_shape=whole,
+        in_specs=[pl.BlockSpec(memory_space=pltpu.VMEM)] * 4,
+        out_specs=pl.BlockSpec(memory_space=pltpu.HBM),
+        scratch_shapes=[plain, dma((CHUNKS,))],
+        compiler_params=pltpu.CompilerParams(vmem_limit_bytes=8 * 1024 * 1024),
+    )(total, on_r, on_w, scale)
 
 
 def solution(mesh):

time: 41.2 us -> 39.6 us (0.961)
  local copies, waits for them, and re-layouts: 0.97 us -> 0 us
  Pallas kernels: 40.1 us -> 39.4 us
    unnamed x1 -> x0, local copies, waits for them, and re-layouts: 0.97 us -> none
    pallas_call x1 -> x2, Pallas kernels: 40.1 us -> 39.4 us  [the longest x1 38.4 us: local(): pl.pallas_call(functools.partial(kernel, gx, gy), out_shape=(whole, whole...]
where the time goes in v3:
time: 39.6 us; the launch traced here: 39.4 us
  Pallas kernels  39.4 us (99%)
    pallas_call x1, Pallas kernels, local(): pl.pallas_call(functools.partial(kernel, gx, gy), out_shape=(whole, whole...  38.4 us
    pallas_call x1, Pallas kernels, local(): pl.pallas_call(finish, out_shape=whole, in_specs=[pl.BlockSpec(memory_spa...  1.04 us

profile of v3, /device:TPU:0, one launch (start us, length us, event | category | flops | bytes accessed | tf_op | source)
XLA Modules:
  0.0 39.4 jit_solution(13378798274701463035)
XLA Ops:
  0.0 38.4 %shard_map.46 = (f32[32,64,128]{2,1,0:T(8,128)S(1)}, f32[32,64,128]{2,1,0:T(8,128)S(1)}, f32[32,64,128]{2,1,0:T(8,128)S(1)}, f32[2,128]{1,0:T(2,128)S(1)}) custom-call(f32[32,64,128]{2,1,0:T(8,128)} %cot_hbm.1, f32[3,32,64,128]{3,2,1,0:T(8,128)} %speed_hbm.1, f32[3,32,64,128]{3,2,1,0:T(8,128)} %coeff_hbm.1, s32[3,32,64]{2,1,0:T(8,128)} %dirs_hbm.1), custom_call_target="tpu_custom_call" | custom-call | tf_op jit(solution)/shard_map/pallas_call | solution.py:654
  38.4 1.0 %shard_map.47 = f32[32,64,128]{2,1,0:T(8,128)} custom-call(f32[32,64,128]{2,1,0:T(8,128)S(1)} %get-tuple-element.9.base, f32[32,64,128]{2,1,0:T(8,128)S(1)} %get-tuple-element.10.on_r, f32[32,64,128]{2,1,0:T(8,128)S(1)} %get-tuple-element.11.on_w, f32[2,128]{1,0:T(2,128)S(1)} %get-tuple-element.12.scale), custom_call_target="tpu_custom_call" | custom-call | tf_op jit(solution)/shard_map/pallas_call | solution.py:692

commit v4 on v3

--- a/solution.py
+++ b/solution.py
@@ -52,8 +52,8 @@
 def kernel(
     gx, gy, cot_hbm, speed_hbm, coeff_hbm, dirs_hbm, out_base, out_r, out_w, out_scale,
     f0, f1, f2, f3, f4, f5, f6, fr0, fr1, fw0, fw1, dw0, dw1, base, cx, cy, cz, czm, px, py, pz, mx, my, mz, gdiag, fdiag,
-    ysend, yrecv, dirs_ref, cx_top, mx_top, cy_top, py_top, landed, wpart, ypart, yside, corner_out, corner_in, slots,
-    load_sem, send_sem, recv_sem, corner_send, corner_recv, sum_send, sum_recv,
+    ysend, yrecv, dirs_ref, c_ends, cx_top, mx_top, cy_top, py_top, landed, wpart, ypart, yside, corner_out, corner_in, slots,
+    load_sem, send_sem, recv_sem, corner_send, corner_recv, sum_send, sum_recv, known,
 ):
     nx, ny, nz = out_base.shape
     fields = (f0, f1, f2, f3, f4, f5, f6)
@@ -83,8 +83,56 @@
         copy.start()
         return copy
 
+    def greet(sem, d):
+        for dx in (-d, 0, d):
+            for dy in (-d, 0, d):
+                if (dx, dy) == (0, 0) or abs(dx) >= gx or abs(dy) >= gy:
+                    continue
+                x, y = me_x + dx, me_y + dy
+                there = jnp.logical_and(jnp.logical_and(x >= 0, x < gx), jnp.logical_and(y >= 0, y < gy))
+
+                @pl.when(there)
+                def _():
+                    pl.semaphore_signal(sem, inc=1, device_id={"gx": x, "gy": y}, device_id_type=MESH)
+
+    def greeted(sem, d):
+        def near(at, size):
+            return 1 + (at >= d).astype(jnp.int32) + (at + d < size).astype(jnp.int32)
+
+        pl.semaphore_wait(sem, near(me_x, gx) * near(me_y, gy) - 1)
+
+    reach = [1]
+    while 2 * reach[-1] < max(gx, gy):
+        reach.append(2 * reach[-1])
+
+    def pass_on(k, last=False):
+        while k < len(reach):
+            greeted(known.at[k], reach[k])
+            k += 1
+            if k < len(reach):
+                greet(known.at[k], reach[k])
+            if not last:
+                break
+
     with jax.named_scope("loads"):
+        plane = jnp.zeros((ny, nz), jnp.float32)
+        for k in range(7):
+            fields[k][0, own] = plane
+            fields[k][nx + 1, own] = plane
+        landed[0] = plane
+        landed[1] = plane
+        yrecv[...] = jnp.zeros_like(yrecv)
+        corner_in[...] = jnp.zeros_like(corner_in)
+
+        barrier = pltpu.get_barrier_semaphore()
+        greet(barrier, 1)
+
         first = 2 + 6 * chunks
+        early = [
+            load(first + 4, cot_hbm.at[0], c_ends.at[0]),
+            load(first + 5, cot_hbm.at[nx - 1], c_ends.at[1]),
+            load(1 + 6 * chunks, dirs_hbm, dirs_ref),
+        ]
         tops = [
             load(first, coeff_hbm.at[0, nx - 1], cx_top),
             load(first + 1, speed_hbm.at[0, nx - 1], mx_top),
@@ -92,7 +140,6 @@
             load(first + 3, speed_hbm.at[1, :, pl.ds(ny - 8, 8)], py_top),
         ]
         cot_load = load(0, cot_hbm, fields[0].at[pl.ds(1, nx), own])
-        dirs_load = load(1 + 6 * chunks, dirs_hbm, dirs_ref)
         loads = []
         for chunk in range(chunks):
             at = pl.ds(chunk * piece, piece)
@@ -108,20 +155,6 @@
                 ))
             ])
 
-        plane = jnp.zeros((ny, nz), jnp.float32)
-        for k in range(7):
-            fields[k][0, own] = plane
-            fields[k][nx + 1, own] = plane
-        landed[0] = plane
-        landed[1] = plane
-        yrecv[...] = jnp.zeros_like(yrecv)
-        corner_in[...] = jnp.zeros_like(corner_in)
-
-        barrier = pltpu.get_barrier_semaphore()
-        for off in range(1, count):
-            to = {"gx": lax.rem(me_x + off // gy, gx), "gy": lax.rem(me_y + off % gy, gy)}
-            pl.semaphore_signal(barrier, inc=1, device_id=to, device_id_type=MESH)
-
         cx[0] = plane
         mx[0] = plane
 
@@ -157,8 +190,9 @@
         field = fields[tag]
         partial = tag > 3
         return (
-            x_down(tag, wpart.at[tag - 4] if partial else field.at[1, own], field.at[nx + 1, own]),
-            x_up(tag, field.at[nx, own], field.at[0, own]),
+            x_down(
+                tag, wpart.at[tag - 4] if partial else field.at[1, own] if tag else c_ends.at[0], field.at[nx + 1, own]),
+            x_up(tag, field.at[nx, own] if tag else c_ends.at[1], field.at[0, own]),
             y_down(tag, ypart.at[tag - 4] if partial else ysend.at[tag, 0]),
             y_up(tag),
         )
@@ -205,36 +239,38 @@
             fields[tag][1 + x, pl.ds(PAD + ny, 1)] = yrecv[tag, 1, pl.ds(x, 1)]
 
     with jax.named_scope("barrier"):
-        cot_load.wait()
-        dirs_load.wait()
+        for copy in early + tops[:2]:
+            copy.wait()
+        dirs = [dirs_ref[d].astype(jnp.float32).T for d in range(3)]
+
+        def upper(d, x):
+            column = (lax.broadcasted_iota(jnp.int32, (nx, nz), 0) == x).astype(jnp.float32)
+            return jnp.dot(dirs[d], column, preferred_element_type=jnp.float32) > 0.5
+
+        mx_top[...] = jnp.where(upper(0, nx - 1), mx_top[...], 0.0)
+        statics = (
+            (x_up(7, cx_top, landed.at[0]), y_up(7)),
+            (x_up(8, mx_top, landed.at[1]), y_up(8)),
+        )
+        greeted(barrier, 1)
+        start(0, XD, XU)
+        greet(known.at[0], reach[0])
+        for xu, _ in statics:
+            pl.when(high_x)(xu.start)
+    with jax.named_scope("rows"):
+        for copy in [cot_load] + tops[2:]:
+            copy.wait()
         for x in range(nx):
             at = pl.ds(x, 1)
             ysend[0, 0, at] = fields[0][x + 1, pl.ds(PAD, 1)]
             ysend[0, 1, at] = fields[0][x + 1, pl.ds(PAD + ny - 1, 1)]
-        dirs = [dirs_ref[d].astype(jnp.float32).T for d in range(3)]
-
-        def upper(d, x):
-            column = (lax.broadcasted_iota(jnp.int32, (nx, nz), 0) == x).astype(jnp.float32)
-            return jnp.dot(dirs[d], column, preferred_element_type=jnp.float32) > 0.5
-
-        for copy in tops:
-            copy.wait()
-        mx_top[...] = jnp.where(upper(0, nx - 1), mx_top[...], 0.0)
-        for x in range(nx):
-            at = pl.ds(x, 1)
             ysend[7, 1, at] = cy_top[x, 7:]
             yside[6, at] = py_top[x, 7:]
         edge = jnp.broadcast_to(dirs_ref[1][:, ny - 1:], (nx, nz)) > 0
         ysend[8, 1] = jnp.where(edge, yside[6], 0.0)
         yside[6] = jnp.where(edge, 0.0, yside[6])
-        pl.semaphore_wait(barrier, count - 1)
-        start(0, YD, YU, XD, XU)
-        statics = (
-            (x_up(7, cx_top, landed.at[0]), y_up(7)),
-            (x_up(8, mx_top, landed.at[1]), y_up(8)),
-        )
-        for xu, yu in statics:
-            pl.when(high_x)(xu.start)
+        start(0, YD, YU)
+        for _, yu in statics:
             pl.when(high_y)(yu.start)
 
     def masks(x, carry):
@@ -268,6 +304,8 @@
             grouped("masks", low, high, masks, store_masks, 0)
         with jax.named_scope("diagonals"):
             grouped("diagonals", low, high, diagonals, store_diagonals, 0)
+
+    pass_on(0)
 
     def spread(ref, x):
         v = ref[x + 1, own]
@@ -468,6 +506,8 @@
         def store_second(x, w):
             keep(w_tag, x, w)
 
+        if step == 0:
+            pass_on(1)
         with jax.named_scope("image"):
             sums = grouped("image", 1, nx - 1, second_pass, store_second, (nothing, nothing))
 
@@ -525,6 +565,8 @@
             m3 += fold(ysend[7, 1] * above * (above - 2.0 * ysend[w_tag, 1]))
             m3 = m2 + implicit_diagonal * m3
         with jax.named_scope("sendsums"):
+            if step == 0:
+                pass_on(2, last=True)
             send_sums(step, (m0, m1, m2, m3))
             start(w_tag, YU, XU)
             for x in range(nx):
@@ -671,6 +713,7 @@
             pltpu.VMEM((9, 2, nx, nz), f32),
             pltpu.VMEM((9, 2, nx, nz), f32),
             pltpu.VMEM(dirs.shape, dirs.dtype),
+            pltpu.VMEM((2, ny, nz), f32),
             pltpu.VMEM((ny, nz), f32),
             pltpu.VMEM((ny, nz), f32),
             pltpu.VMEM((nx, 8, nz), f32),
@@ -682,8 +725,9 @@
             pltpu.VMEM((3, 4, 1, nz), f32),
             pltpu.VMEM((3, 4, 1, nz), f32),
             pltpu.VMEM((3, gx * gy, 1, nz), f32),
-            dma((6 + 6 * CHUNKS,)), dma((9, 4)), dma((9, 4)),
+            dma((8 + 6 * CHUNKS,)), dma((9, 4)), dma((9, 4)),
             dma((3, 3)), dma((3, 3)), dma((3,)), dma((3,)),
+            pltpu.SemaphoreType.REGULAR((max(gx, gy).bit_length(),)),
         ],
         compiler_params=pltpu.CompilerParams(
             collective_id=0, has_side_effects=True, vmem_limit_bytes=46 * 1024 * 1024

time: 39.6 us -> 39.1 us (0.987)
  Pallas kernels: 39.4 us -> 38.8 us
    pallas_call x1, Pallas kernels: 38.4 us -> 37.8 us  [local(): pl.pallas_call(functools.partial(kernel, gx, gy), out_shape=(whole, whole...]
where the time goes in v4:
time: 39.1 us; the launch traced here: 39 us
  Pallas kernels  38.8 us (99%)
    pallas_call x1, Pallas kernels, local(): pl.pallas_call(functools.partial(kernel, gx, gy), out_shape=(whole, whole...  37.8 us
    pallas_call x1, Pallas kernels, local(): pl.pallas_call(finish, out_shape=whole, in_specs=[pl.BlockSpec(memory_spa...  1.04 us

profile of v4, /device:TPU:0, one launch (start us, length us, event | category | flops | bytes accessed | tf_op | source)
XLA Modules:
  0.0 39.0 jit_solution(3040153024284838185)
XLA Ops:
  0.0 37.8 %shard_map.46 = (f32[32,64,128]{2,1,0:T(8,128)S(1)}, f32[32,64,128]{2,1,0:T(8,128)S(1)}, f32[32,64,128]{2,1,0:T(8,128)S(1)}, f32[2,128]{1,0:T(2,128)S(1)}) custom-call(f32[32,64,128]{2,1,0:T(8,128)} %cot_hbm.1, f32[3,32,64,128]{3,2,1,0:T(8,128)} %speed_hbm.1, f32[3,32,64,128]{3,2,1,0:T(8,128)} %coeff_hbm.1, s32[3,32,64]{2,1,0:T(8,128)} %dirs_hbm.1), custom_call_target="tpu_custom_call" | custom-call | tf_op jit(solution)/shard_map/pallas_call | solution.py:696
  37.8 1.0 %shard_map.47 = f32[32,64,128]{2,1,0:T(8,128)} custom-call(f32[32,64,128]{2,1,0:T(8,128)S(1)} %get-tuple-element.9.base, f32[32,64,128]{2,1,0:T(8,128)S(1)} %get-tuple-element.10.on_r, f32[32,64,128]{2,1,0:T(8,128)S(1)} %get-tuple-element.11.on_w, f32[2,128]{1,0:T(2,128)S(1)} %get-tuple-element.12.scale), custom_call_target="tpu_custom_call" | custom-call | tf_op jit(solution)/shard_map/pallas_call | solution.py:736

commit v5 on v4

--- a/solution.py
+++ b/solution.py
@@ -26,7 +26,7 @@
 PAD = 8
 
 
-GROUP = {"masks": 8, "diagonals": 8, "source": 15, "strip": 29, "next": 29, "image": 10, "energy": 14, "rim": 28, "carry": 16, "both": 8, "gather": 16, "last": 8}
+GROUP = {"masks": 8, "diagonals": 8, "source": 16, "strip": 29, "next": 29, "image": 10, "energy": 14, "rim": 28, "carry": 16, "both": 8, "gather": 16, "last": 8}
 CHUNKS = 4
 
 
@@ -424,54 +424,57 @@
         m0 = nothing
         if step == 0:
             with jax.named_scope("first"):
-                m0 = grouped("source", 2, nx - 1, first_pass, store_first, m0)
+                m0 = grouped("source", 1, nx - 1, first_pass, store_first, m0)
             with jax.named_scope("arrive0"):
                 arrive(0, XD, XU, YD, YU)
-                for x in outer:
-                    fields[0][1 + x, pl.ds(PAD - 1, 1)] = yrecv[0, 0, pl.ds(x, 1)]
-                    fields[0][1 + x, pl.ds(PAD + ny, 1)] = yrecv[0, 1, pl.ds(x, 1)]
+                m0, kept = first_pass(nx - 1, m0)
+                store_first(nx - 1, kept)
+                fields[0][1, pl.ds(PAD - 1, 1)] = yrecv[0, 0, pl.ds(0, 1)]
+                fields[0][1, pl.ds(PAD + ny, 1)] = yrecv[0, 1, pl.ds(0, 1)]
             with jax.named_scope("statics"):
                 for xu, yu in statics:
                     pl.when(low_x)(xu.wait_recv)
                     pl.when(low_y)(yu.wait_recv)
+            head = pl.ds(0, 1)
+            with jax.named_scope("firstedge"):
+                for side, change in (
+                    (0, (yrecv[7, 0] + yrecv[8, 0]) * (yrecv[0, 0] - ysend[0, 0])),
+                    (1, (ysend[7, 1] + yside[6]) * yrecv[0, 1]),
+                ):
+                    change = jnp.where(row_x > 0, section_weights[3] * change, 0.0)
+                    r = jnp.where(row_x > 0, ysend[r_tag, side], 0.0)
+                    m0 += fold((2.0 * r + change) * change)
+                    ysend[r_tag, side] = r + change
+                for x in range(1, nx):
+                    r_ref[1 + x, pl.ds(PAD, 1)] = ysend[r_tag, 0, pl.ds(x, 1)]
+                    r_ref[1 + x, pl.ds(PAD + ny - 1, 1)] = ysend[r_tag, 1, pl.ds(x, 1)]
                 cx[0] = landed[0]
                 mx[0] = landed[1]
                 gdiag[0] += cx[0]
                 fdiag[0] += mx[0]
-                head = pl.ds(0, 1)
+                cy[0, pl.ds(PAD - 1, 1)] = yrecv[7, 0, head]
+                my[0, pl.ds(PAD - 1, 1)] = yrecv[8, 0, head]
+                gdiag[0, head] += yrecv[7, 0, head]
+                fdiag[0, head] += yrecv[8, 0, head]
+                m0, kept = first_pass(0, m0)
+                store_first(0, kept)
+                send_x()
+                start(r_tag, YD, YU)
+            with jax.named_scope("patch"):
                 for x in range(nx):
                     at = pl.ds(x, 1)
-                    row = yrecv[7, 0, at]
-                    cy[x, pl.ds(PAD - 1, 1)] = row
-                    g = gdiag[x, head] + row
-                    gdiag[x, head] = g
-                    yside[3, at] = g
-                    row = yrecv[8, 0, at]
-                    my[x, pl.ds(PAD - 1, 1)] = row
-                    fdiag[x, head] += row
+                    if x:
+                        row = yrecv[7, 0, at]
+                        cy[x, pl.ds(PAD - 1, 1)] = row
+                        gdiag[x, head] += row
+                        row = yrecv[8, 0, at]
+                        my[x, pl.ds(PAD - 1, 1)] = row
+                        fdiag[x, head] += row
+                    yside[3, at] = gdiag[x, head]
                     yside[0, at] = cx[x + 1, head] if x < nx - 1 else jnp.zeros((1, nz), jnp.float32)
                     yside[4, at] = cx[x, head] if x else jnp.zeros((1, nz), jnp.float32)
                     yside[1, at] = cy[x, pl.ds(PAD, 1)]
                     yside[2, at] = czm[x, head]
-            with jax.named_scope("firstedge"):
-                for x in outer:
-                    m0, kept = first_pass(x, m0)
-                    store_first(x, kept)
-                send_x()
-            with jax.named_scope("patch"):
-                inside = jnp.logical_and(row_x > 1, row_x < nx - 1)
-                for side, change in (
-                    (0, (yrecv[7, 0] + yrecv[8, 0]) * (yrecv[0, 0] - ysend[0, 0])),
-                    (1, (ysend[7, 1] + yside[6]) * yrecv[0, 1]),
-                ):
-                    change = jnp.where(inside, section_weights[3] * change, 0.0)
-                    r = ysend[r_tag, side]
-                    m0 += fold((2.0 * r + change) * change)
-                    ysend[r_tag, side] = r + change
-                for x in range(2, nx - 1):
-                    r_ref[1 + x, pl.ds(PAD, 1)] = ysend[r_tag, 0, pl.ds(x, 1)]
-                    r_ref[1 + x, pl.ds(PAD + ny - 1, 1)] = ysend[r_tag, 1, pl.ds(x, 1)]
-                start(r_tag, YD, YU)
         else:
             with jax.named_scope("firstedge"):
                 value, store = part(0, ny)
@@ -639,10 +642,11 @@
         with jax.named_scope("allsums"):
             m0, m1, m2, m3 = read_sums(step)
         alpha = m0 / m1
+        beyond = m1 / m0
         rr = alpha * alpha * m2 - m0
-        ratio = rr / m0
+        ratio = rr * (1.0 / m0)
         product = m1 - 2.0 * alpha * m2 + alpha * alpha * m3
-        alpha_next = rr / (product - ratio * rr / alpha)
+        alpha_next = rr / (product - ratio * rr * beyond)
         on_r = alpha + alpha_next * (1.0 + ratio)
         on_w = -alpha_next * alpha
         weights.append((on_r, on_w))

time: 39.1 us -> 39 us (level)
  no operation moved by 1% of the time
where the time goes in v5:
time: 39 us; the launch traced here: 38.8 us
  Pallas kernels  38.7 us (99%)
    pallas_call x1, Pallas kernels, local(): pl.pallas_call(functools.partial(kernel, gx, gy), out_shape=(whole, whole...  37.6 us
    pallas_call x1, Pallas kernels, local(): pl.pallas_call(finish, out_shape=whole, in_specs=[pl.BlockSpec(memory_spa...  1.04 us

profile of v5, /device:TPU:0, one launch (start us, length us, event | category | flops | bytes accessed | tf_op | source)
XLA Modules:
  0.0 38.8 jit_solution(5544284190040433171)
XLA Ops:
  0.0 37.6 %shard_map.46 = (f32[32,64,128]{2,1,0:T(8,128)S(1)}, f32[32,64,128]{2,1,0:T(8,128)S(1)}, f32[32,64,128]{2,1,0:T(8,128)S(1)}, f32[2,128]{1,0:T(2,128)S(1)}) custom-call(f32[32,64,128]{2,1,0:T(8,128)} %cot_hbm.1, f32[3,32,64,128]{3,2,1,0:T(8,128)} %speed_hbm.1, f32[3,32,64,128]{3,2,1,0:T(8,128)} %coeff_hbm.1, s32[3,32,64]{2,1,0:T(8,128)} %dirs_hbm.1), custom_call_target="tpu_custom_call" | custom-call | tf_op jit(solution)/shard_map/pallas_call | solution.py:700
  37.6 1.0 %shard_map.47 = f32[32,64,128]{2,1,0:T(8,128)} custom-call(f32[32,64,128]{2,1,0:T(8,128)S(1)} %get-tuple-element.9.base, f32[32,64,128]{2,1,0:T(8,128)S(1)} %get-tuple-element.10.on_r, f32[32,64,128]{2,1,0:T(8,128)S(1)} %get-tuple-element.11.on_w, f32[2,128]{1,0:T(2,128)S(1)} %get-tuple-element.12.scale), custom_call_target="tpu_custom_call" | custom-call | tf_op jit(solution)/shard_map/pallas_call | solution.py:740

commit v6 on v5

--- a/solution.py
+++ b/solution.py
@@ -26,7 +26,7 @@
 PAD = 8
 
 
-GROUP = {"masks": 8, "diagonals": 8, "source": 16, "strip": 29, "next": 29, "image": 10, "energy": 14, "rim": 28, "carry": 16, "both": 8, "gather": 16, "last": 8}
+GROUP = {"masks": 8, "diagonals": 8, "source": 10, "strip": 29, "next": 29, "image": 10, "energy": 14, "rim": 28, "carry": 16, "both": 8, "gather": 16, "last": 8}
 CHUNKS = 4
 
 

time: 39 us -> 38.8 us (level)
  no operation moved by 1% of the time
where the time goes in v6:
time: 38.8 us; the launch traced here: 38.7 us
  Pallas kernels  38.7 us (100%)
    pallas_call x1, Pallas kernels, local(): pl.pallas_call(functools.partial(kernel, gx, gy), out_shape=(whole, whole...  37.6 us
    pallas_call x1, Pallas kernels, local(): pl.pallas_call(finish, out_shape=whole, in_specs=[pl.BlockSpec(memory_spa...  1.04 us

profile of v6, /device:TPU:0, one launch (start us, length us, event | category | flops | bytes accessed | tf_op | source)
XLA Modules:
  0.0 38.7 jit_solution(15845034095923004177)
XLA Ops:
  0.0 37.6 %shard_map.46 = (f32[32,64,128]{2,1,0:T(8,128)S(1)}, f32[32,64,128]{2,1,0:T(8,128)S(1)}, f32[32,64,128]{2,1,0:T(8,128)S(1)}, f32[2,128]{1,0:T(2,128)S(1)}) custom-call(f32[32,64,128]{2,1,0:T(8,128)} %cot_hbm.1, f32[3,32,64,128]{3,2,1,0:T(8,128)} %speed_hbm.1, f32[3,32,64,128]{3,2,1,0:T(8,128)} %coeff_hbm.1, s32[3,32,64]{2,1,0:T(8,128)} %dirs_hbm.1), custom_call_target="tpu_custom_call" | custom-call | tf_op jit(solution)/shard_map/pallas_call | solution.py:700
  37.6 1.0 %shard_map.47 = f32[32,64,128]{2,1,0:T(8,128)} custom-call(f32[32,64,128]{2,1,0:T(8,128)S(1)} %get-tuple-element.9.base, f32[32,64,128]{2,1,0:T(8,128)S(1)} %get-tuple-element.10.on_r, f32[32,64,128]{2,1,0:T(8,128)S(1)} %get-tuple-element.11.on_w, f32[2,128]{1,0:T(2,128)S(1)} %get-tuple-element.12.scale), custom_call_target="tpu_custom_call" | custom-call | tf_op jit(solution)/shard_map/pallas_call | solution.py:740
